TPU v7x, 32 devices: a whole 2x2x4 slice. The times are simulated.
32 devices in a mesh: dp: 2 (over x), tp: 16 (over z, y, core).
Axes of the slice: x: 2, y: 2, z: 4, core: 2. Of those that a mesh axis runs over, the one named last changes fastest.
Arguments:
- hidden: bfloat16 [4096, 2048], P(('dp', 'tp')), parts along dimension 0
- w_two: bfloat16 [2048, 2048], replicated
- ln_scale: float32 [2, 2048], replicated
- ln_shift: float32 [2, 2048], replicated
- embed: bfloat16 [49152, 2048], P('tp')
- targets: int32 [2, 4096], P(None, ('dp', 'tp')), parts along dimension 1
- loss_mask: int32 [2, 4096], P(None, ('dp', 'tp')), parts along dimension 1
Outputs:
- output 1: float32 [2, 4096], P(None, ('dp', 'tp')), parts along dimension 1
- output 2: float32 [2], P('dp'), parts along dimension 0
- output 3: bfloat16 [4096, 2048], P(('dp', 'tp')), parts along dimension 0
- output 4: float32 [98304, 2048], P(('dp', 'tp')), parts along dimension 0
- output 5: float32 [4096, 2048], P('dp'), parts along dimension 0
- output 6: float32 [4, 2048], P('dp'), parts along dimension 0
- output 7: float32 [4, 2048], P('dp'), parts along dimension 0
There are 2 independent parts. A program takes and returns all parts, laid end to end along the dimension named above; an argument that names none is the same for every part.
All inputs are finite; a program needn't handle non-finite values.
Results may differ from a plain program's by a relative error of at most 0.0017.
Values are sent between devices in bfloat16 or wider.
A program may use at most 1 GiB of HBM per device.

v0:
```python
import jax
import jax.numpy as jnp
from jax import lax
from jax.sharding import PartitionSpec as P

LN_EPS = 1e-5


def layer_norm(values, gain, bias):
    mean_val = jnp.mean(values, axis=-1, keepdims=True)
    centered = values - mean_val
    variance = jnp.mean(centered * centered, axis=-1, keepdims=True)
    return centered * lax.rsqrt(variance + LN_EPS) * gain + bias


def solution(mesh):
    tok_spec = P(('dp', 'tp'), None)
    row_spec = P(None, ('dp', 'tp'))

    def device_step(hidden, w_two, ln_scale, ln_shift, embed, targets, loss_mask):
        tok_rows = hidden.shape[0]
        shard_rows = embed.shape[0]
        shard_idx = lax.axis_index('tp')
        proj_out = jnp.dot(hidden, w_two, preferred_element_type=jnp.float32).astype(jnp.bfloat16)
        norm_input = jnp.stack([hidden.astype(jnp.float32), proj_out.astype(jnp.float32)])
        normed, ln_back = jax.vjp(jax.vmap(layer_norm), norm_input, ln_scale, ln_shift)
        x_loc = normed.astype(jnp.bfloat16)
        x_all = lax.all_gather(x_loc, 'tp', axis=1, tiled=True)
        int_all = lax.all_gather(jnp.stack([targets, loss_mask]), 'tp', axis=2, tiled=True)
        tgt_all = int_all[0]
        mask_all = int_all[1].astype(jnp.float32)
        logits = jnp.einsum('hsd,vd->hsv', x_all, embed, preferred_element_type=jnp.float32)
        local_max = jnp.max(logits, axis=-1)
        exp_loc = jnp.exp(logits - local_max[..., None])
        col_ids = lax.broadcasted_iota(jnp.int32, (1, 1, shard_rows), 2) + shard_idx * shard_rows
        is_target = col_ids == tgt_all[..., None]
        tgt_loc = jnp.sum(jnp.where(is_target, logits, 0.0), axis=-1)
        glob_max = lax.pmax(local_max, 'tp')
        part_stats = jnp.stack([jnp.sum(exp_loc, axis=-1) * jnp.exp(local_max - glob_max), tgt_loc])
        glob_stats = lax.psum(part_stats, 'tp')
        log_norm = glob_max + jnp.log(glob_stats[0])
        token_count = jnp.sum(mask_all, axis=1)
        weight = mask_all / token_count[:, None]
        loss_all = (log_norm - glob_stats[1]) * mask_all
        total_loss = jnp.sum(loss_all / token_count[:, None]).reshape(1)
        token_loss = lax.dynamic_slice_in_dim(loss_all, shard_idx * tok_rows, tok_rows, axis=1)
        softmax_val = exp_loc * jnp.exp(local_max - log_norm)[..., None]
        d_logits = (jnp.where(is_target, softmax_val - 1.0, softmax_val) * weight[..., None]).astype(jnp.bfloat16)
        d_embed = jnp.einsum('hsv,hsd->vd', d_logits, x_all, preferred_element_type=jnp.float32)
        dx_part = jnp.einsum('hsv,vd->hsd', d_logits, embed, preferred_element_type=jnp.float32)
        dx_loc = lax.psum_scatter(dx_part, 'tp', scatter_dimension=1, tiled=True)
        d_norm_in, d_scale_part, d_shift_part = ln_back(dx_loc)
        d_proj = d_norm_in[1].astype(jnp.bfloat16)
        d_hidden = (d_norm_in[0] + jnp.einsum('td,ed->te', d_proj, w_two, preferred_element_type=jnp.float32)).astype(jnp.bfloat16)
        d_w_part = jnp.einsum('te,td->ed', hidden, d_proj, preferred_element_type=jnp.float32)
        d_w_two, d_scale, d_shift = lax.psum((d_w_part, d_scale_part, d_shift_part), 'tp')
        return token_loss, total_loss, d_hidden, d_embed, d_w_two, d_scale, d_shift

    return jax.shard_map(device_step, mesh=mesh,
                         in_specs=(tok_spec, P(), P(), P(), P('tp', None), row_spec, row_spec),
                         out_specs=(row_spec, P('dp'), tok_spec, tok_spec, P('dp', None), P('dp', None), P('dp', None)),
                         check_vma=False)
```

profile of v0, /device:TPU:0, one launch (start us, length us, event | category | flops | bytes accessed | tf_op | source)
XLA Modules:
  0.0 1077.4 jit_solution(18053524774435911489)
XLA Ops:
  7.2 0.0 copy-start
  7.2 0.0 copy-start.6
  7.2 0.0 copy-start.22
  7.2 0.0 copy-start.23
  7.2 0.0 all-gather.2.cloned.1.call-start
  7.3 4.9 fusion.15
  12.1 0.0 copy-start.2
  12.2 0.2 convert_reduce_fusion
  12.4 0.4 fusion.19
  12.8 0.5 copy-done.19
  13.4 0.0 copy-done.2
  13.4 0.0 copy-start.16
  13.4 0.6 copy-done.16
  14.0 1.5 fusion.17
  15.4 0.0 all-gather.2.cloned.1.call-update
  15.5 0.0 reduce-scatter.2.cloned.1.call-start
  15.5 0.0 copy-done.22
  15.5 0.0 copy-done.23
  15.5 23.3 %all_gather.7 = s32[2,2,2048]{2,1,0:T(2,128)S(1)} all-gather(s32[2,2,128]{2,1,0:T(2,128)S(1)} %pad_add_fusion), channel_id=1, replica_groups=mesh['dp'=2,'tp'=16] {'tp'}, dimensions={2}, use_global_device_ids=true | all-gather | bytes 34816 | tf_op jit(solution)/shard_map/all_gather | solution.py:29
  38.9 0.6 iota_add_fusion
  39.5 0.6 fusion.29
  40.1 0.6 slice_bitcast_fusion.2
  40.7 103.4 %all-gather.2.cloned.1.call-done = bf16[2,2048,2048]{2,1,0:T(8,128)(2,1)} async-done(((bf16[2,128,2048]{2,1,0:T(8,128)(2,1)}), bf16[2,2048,2048]{2,1,0:T(8,128)(2,1)}) %all-gather.2.cloned.1.call-update) | async-done | bytes 16777232 | tf_op jit(solution)/shard_map/all_gather | solution.py:28
  144.2 62.2 %fusion.35 = (f32[2,2048]{1,0:T(2,128)S(1)}, f32[2,2048,3072]{2,1,0:T(8,128)}) fusion(bf16[2,2048,2048]{2,1,0:T(8,128)(2,1)} %all-gather.2.cloned.1.call-done, bf16[3072,2048]{1,0:T(8,128)(2,1)} %param.11), kind=kOutput, calls=%fused_computation.60 | convolution fusion | flops 51552186368 | bytes 79708160 | tf_op jit(solution)/shard_map/hsd,vd->hsv/dot_general | solution.py:32
  206.3 59.3 %pmax.7 = f32[2,2048]{1,0:T(2,128)S(1)} all-reduce(f32[2,2048]{1,0:T(2,128)S(1)} %get-tuple-element.26), channel_id=1, replica_groups=mesh['dp'=2,'tp'=16] {'tp'}, use_global_device_ids=true, to_apply=%region_3.4 | all-reduce | flops 4096 | bytes 32768 | tf_op jit(solution)/shard_map/pmax | solution.py:38
  265.6 0.0 copy-done.13
  265.6 22.3 %fusion.3 = (f32[2,2048]{1,0:T(2,128)S(1)}, f32[2,2048]{1,0:T(2,128)S(1)}) fusion(f32[2,2048,3072]{2,1,0:T(8,128)} %get-tuple-element.27, f32[2,2048]{1,0:T(2,128)S(1)} %get-tuple-element.26, s32[2,2048]{1,0:T(2,128)S(1)} %copy-done.10, s32[3072]{0:T(1024)S(1)} %copy-done.13), kind=kLoop, calls=%fused_computation.6 | loop fusion | flops 62906368 | bytes 50409472 | tf_op jit(solution)/shard_map/reduce_sum | solution.py:39
  288.0 57.6 %psum.28 = f32[2,2,2048]{2,1,0:T(2,128)S(1)} all-reduce(f32[2,2,2048]{2,1,0:T(2,128)S(1)} %pad_maximum_fusion.1), channel_id=1, replica_groups=mesh['dp'=2,'tp'=16] {'tp'}, use_global_device_ids=true, to_apply=%region_6.7 | all-reduce | flops 8192 | bytes 65536 | tf_op jit(solution)/shard_map/psum | solution.py:40
  345.6 1.2 divide_reduce_fusion
  346.8 64.5 %fusion.4 = f32[2,2048,2048]{2,1,0:T(8,128)} fusion(bf16[3072,2048]{1,0:T(8,128)(2,1)} %param.11, f32[2,2048,3072]{2,1,0:T(8,128)} %get-tuple-element.27, f32[2,2048]{1,0:T(2,128)S(1)} %get-tuple-element.25, f32[2,2048]{1,0:T(2,128)S(1)} %get-tuple-element.24, s32[2,2048]{1,0:T(2,128)S(1)} %copy-done.10, s32[3072]{0:T(1024)S(1)} %copy-done.13, ...), kind=kOutput, calls=%fused_computation.8 | convolution fusion | flops 51627687936 | bytes 96546816 | tf_op jit(solution)/shard_map/hsv,vd->hsd/dot_general | solution.py:50
  411.3 0.0 reduce-scatter.2.cloned.1.call-update
  411.4 0.3 all-reduce.3.cloned.1.call-start
  411.6 1.2 constant_dynamic-slice_fusion
  412.9 324.1 %reduce-scatter.2.cloned.1.call-done = f32[2,128,2048]{2,1,0:T(8,128)} async-done(((f32[2,2048,2048]{2,1,0:T(8,128)}), f32[2,128,2048]{2,1,0:T(8,128)}) %reduce-scatter.2.cloned.1.call-update) | async-done | bytes 2097168 | tf_op jit(solution)/shard_map/reduce_scatter | solution.py:51
  737.0 0.0 copy-done.3
  737.0 2.8 fusion.33
  739.8 3.1 fusion.18
  742.9 2.2 broadcast_add_fusion
  745.2 1.3 copy-done.4
  746.5 8.5 convolution_bitcast_fusion.1
  755.0 0.0 all-reduce.3.cloned.1.call-update
  755.1 0.0 copy-start.11
  755.1 0.0 copy-start.12
  755.1 81.9 %convolution_bitcast_fusion = f32[3072,2048]{1,0:T(8,128)} fusion(bf16[2,2048,2048]{2,1,0:T(8,128)(2,1)} %all-gather.2.cloned.1.call-done, f32[2,2048,3072]{2,1,0:T(8,128)} %get-tuple-element.27, f32[2,2048]{1,0:T(2,128)S(1)} %get-tuple-element.25, f32[2,2048]{1,0:T(2,128)S(1)} %get-tuple-element.24, s32[2,2048]{1,0:T(2,128)S(1)} %copy-done.10, ...), kind=kOutput, calls=%fused_computation.7 | convolution fusion | flops 51627687936 | bytes 92352512 | tf_op jit(solution)/shard_map/hsv,hsd->vd/dot_general | solution.py:49
  837.0 61.2 %all-reduce = (f32[2,2048]{1,0:T(2,128)}, f32[2,2048]{1,0:T(2,128)}) all-reduce(f32[2,2048]{1,0:T(2,128)S(1)} %copy-done.12, f32[2,2048]{1,0:T(2,128)S(1)} %copy-done.11), channel_id=1, replica_groups=mesh['dp'=2,'tp'=16] {'tp'}, use_global_device_ids=true, to_apply=%region_14.15 | all-reduce | flops 8192 | bytes 65536 | tf_op jit(solution)/shard_map/psum | solution.py:56
  898.2 7.1 fusion.12
  905.2 148.0 %all-reduce.3.cloned.1.call-done = f32[2048,2048]{0,1:T(8,128)} async-done(((f32[2048,2048]{0,1:T(8,128)}), f32[2048,2048]{0,1:T(8,128)}) %all-reduce.3.cloned.1.call-update) | async-done | bytes 16777232 | tf_op jit(solution)/shard_map/psum | solution.py:56
  1053.3 17.6 %copy.15 = f32[2048,2048]{1,0:T(8,128)} copy(f32[2048,2048]{0,1:T(8,128)} %all-reduce.3.cloned.1.call-done) | data formatting | bytes 33554432
  (39 shorter events, 0.1 us)
Async XLA Ops:
  7.2 5.0 copy-start
  7.2 6.8 copy-start.18
  7.2 6.8 copy-start.6
  7.2 8.3 copy-start.22
  7.2 8.3 copy-start.23
  7.2 136.9 %all-gather.2.cloned.1.call-start = ((), (), s32[]{:S(2)}) async-start(), calls=%async_computation.1 | async-start | bytes 17825792 | tf_op jit(solution)/shard_map/all_gather | solution.py:28
  12.1 1.2 copy-start.2
  12.4 1.0 copy-start.14
  12.8 0.5 copy-start.19
  13.4 0.6 copy-start.16
  15.5 721.5 %reduce-scatter.2.cloned.1.call-start = ((), (), s32[]{:S(2)}) async-start(), calls=%async_computation.2 | async-start | bytes 35651584 | tf_op jit(solution)/shard_map/reduce_scatter | solution.py:51
  38.9 1.3 copy-start.8
  144.2 121.5 %copy-start.10 = (s32[2,2048]{1,0:T(2,128)S(1)}, s32[2,2048]{1,0:T(2,128)}, u32[]{:S(2)}) copy-start(s32[2,2048]{1,0:T(2,128)} %slice_bitcast_fusion.2) | copy-start | bytes 49156
  144.2 121.5 %copy-start.13 = (s32[3072]{0:T(1024)S(1)}, s32[3072]{0:T(1024)}, u32[]{:S(2)}) copy-start(s32[3072]{0:T(1024)} %iota_add_fusion) | copy-start | bytes 36868
  265.6 79.9 %copy-start.9 = (s32[2,2,2048]{2,1,0:T(2,128)S(1)}, s32[2,2,2048]{2,1,0:T(2,128)}, u32[]{:S(2)}) copy-start(s32[2,2,2048]{2,1,0:T(2,128)} %copy-done.8) | copy-start | bytes 98308
  265.6 79.9 %copy-start.21 = (f32[2]{0:T(128)S(1)}, f32[2]{0:T(128)}, u32[]{:S(2)}) copy-start(f32[2]{0:T(128)} %fusion.29) | copy-start | bytes 28
  411.3 325.7 %copy-start.1 = (bf16[128,2048]{1,0:T(8,128)(2,1)S(1)}, bf16[128,2048]{1,0:T(8,128)(2,1)}, u32[]{:S(2)}) copy-start(bf16[128,2048]{1,0:T(8,128)(2,1)} %param.7) | copy-start | bytes 1572868
  411.3 325.7 %copy-start.3 = (bf16[1,128,2048]{2,1,0:T(8,128)(2,1)S(1)}, bf16[1,128,2048]{2,1,0:T(8,128)(2,1)}, u32[]{:S(2)}) copy-start(bf16[1,128,2048]{2,1,0:T(8,128)(2,1)} %copy-done.2) | copy-start | bytes 1572868
  411.3 325.7 %copy-start.7 = (f32[2,2048]{1,0:T(2,128)S(1)}, f32[2,2048]{1,0:T(2,128)}, u32[]{:S(2)}) copy-start(f32[2,2048]{1,0:T(2,128)} %param.9) | copy-start | bytes 49156
  411.3 325.7 %copy-start.15 = (f32[2,128]{1,0:T(2,128)S(1)}, f32[2,128]{1,0:T(2,128)}, u32[]{:S(2)}) copy-start(f32[2,128]{1,0:T(2,128)} %copy-done.14) | copy-start | bytes 3076
  411.3 328.5 %copy-start.20 = (f32[2,128]{1,0:T(2,128)S(1)}, f32[2,128]{1,0:T(2,128)}, u32[]{:S(2)}) copy-start(f32[2,128]{1,0:T(2,128)} %copy-done.19) | copy-start | bytes 3076
  411.3 328.5 %copy-start.17 = (f32[2,128]{1,0:T(2,128)S(1)}, f32[2,128]{1,0:T(2,128)}, u32[]{:S(2)}) copy-start(f32[2,128]{1,0:T(2,128)} %copy-done.16) | copy-start | bytes 3076
  411.4 641.9 %all-reduce.3.cloned.1.call-start = ((), (), s32[]{:S(2)}) async-start(), calls=%async_computation.3 | async-start | bytes 33554432 | tf_op jit(solution)/shard_map/psum | solution.py:56
  745.2 1.3 copy-start.4
  755.1 82.0 %copy-start.11 = (f32[2,2048]{1,0:T(2,128)S(1)}, f32[2,2048]{1,0:T(2,128)}, u32[]{:S(2)}) copy-start(f32[2,2048]{1,0:T(2,128)} %get-tuple-element.18) | copy-start | bytes 49156
  755.1 81.9 %copy-start.12 = (f32[2,2048]{1,0:T(2,128)S(1)}, f32[2,2048]{1,0:T(2,128)}, u32[]{:S(2)}) copy-start(f32[2,2048]{1,0:T(2,128)} %get-tuple-element.16) | copy-start | bytes 49156
  755.1 143.1 %copy-start.5 = (f32[2,128,2048]{2,1,0:T(8,128)S(1)}, f32[2,128,2048]{2,1,0:T(8,128)}, u32[]{:S(2)}) copy-start(f32[2,128,2048]{2,1,0:T(8,128)} %copy-done.4) | copy-start | bytes 6291460
Sparse Core Ops, SparseCore 0:
  15.6 128.5 all-gather.1
  411.5 325.4 reduce-scatter.1
  755.2 298.0 all-reduce.2
where the time goes:
time: 1080 us
  waiting for transfers between devices  576 us (53%)
  matrix products  229 us (21%)
  blocking collectives  201 us (19%)
  other arithmetic  35.1 us (3%)
  local copies, waits for them, and re-layouts  22 us (2%)
  between operations  14 us (1%)
    reduce_scatter x1, waiting for transfers between devices, device_step(): dx_loc = lax.psum_scatter(dx_part, 'tp', scatter_dimension=1, tiled=True)  324 us
    psum x1, waiting for transfers between devices, device_step(): lax.psum((d_w_part, d_scale_part, d_shift_part), 'tp')  148 us
    all_gather x1, waiting for transfers between devices, device_step(): x_all = lax.all_gather(x_loc, 'tp', axis=1, tiled=True)  103 us
    dot_general x1, matrix products, device_step(): jnp.einsum('hsv,hsd->vd', d_logits, x_all, preferred_element_type=jnp.flo...  81.9 us
    dot_general x1, matrix products, device_step(): jnp.einsum('hsv,vd->hsd', d_logits, embed, preferred_element_type=jnp.flo...  64.5 us
    dot_general x1, matrix products, device_step(): jnp.einsum('hsd,vd->hsv', x_all, embed, preferred_element_type=jnp.float32)  62.2 us
    psum x1, blocking collectives, device_step(): lax.psum((d_w_part, d_scale_part, d_shift_part), 'tp')  61.2 us
    pmax x1, blocking collectives, device_step(): glob_max = lax.pmax(local_max, 'tp')  59.3 us
  transfers between devices with their start and end apart: 3, of which 3 were waited for; matrix products, arithmetic and copies ran while one was open for 9% of the time, Pallas kernels for 0%

commit v1 on v0

v1 whole, which is shorter than its diff:
```python
import functools
import jax
import jax.numpy as jnp
from jax import lax
from jax.experimental import pallas as pl
from jax.experimental.pallas import tpu as pltpu
from jax.sharding import PartitionSpec as P

LN_EPS = 1e-5
F32 = jnp.float32
BF = jnp.bfloat16
MESH = pl.DeviceIdType.MESH
VMEM_LIMIT = 56 * 1024 * 1024

ALL = [(z, y, c) for z in range(4) for y in range(2) for c in range(2)]


def tp_of(z, y, c):
    return z * 4 + y * 2 + c


CORE_PAIRS = [(tp_of(z, y, c), tp_of(z, y, 1 - c)) for z, y, c in ALL]
Y_PAIRS = [(tp_of(z, y, c), tp_of(z, 1 - y, c)) for z, y, c in ALL]
Z_PAIRS = {k: [(tp_of(z, y, c), tp_of((z + k) % 4, y, c)) for z, y, c in ALL] for k in (1, 2, 3)}


def place():
    me = lax.axis_index('tp')
    return lax.div(me, 4), lax.rem(lax.div(me, 2), 2), lax.rem(me, 2)


def remote(src, dst, send_sem, recv_sem, dev):
    return pltpu.make_async_remote_copy(src_ref=src, dst_ref=dst, send_sem=send_sem, recv_sem=recv_sem,
                                        device_id={'tp': dev}, device_id_type=MESH)


def small_gather_body(x_ref, o_ref, send, recv):
    z, y, c = place()
    barrier = pltpu.get_barrier_semaphore()
    peers = [(r, k) for r in range(4) for k in range(4) if (r, k) != (0, 0)]

    def peer(r, k):
        pz, py, pc = lax.rem(z + k, 4), lax.rem(y + r % 2, 2), lax.rem(c + r // 2, 2)
        return pz, 2 * pc + py, tp_of(pz, py, pc)

    for r, k in peers:
        pl.semaphore_signal(barrier, inc=1, device_id={'tp': peer(r, k)[2]}, device_id_type=MESH)
    pl.semaphore_wait(barrier, len(peers))
    mine = o_ref.at[2 * c + y, z]
    copies = [remote(x_ref, mine, send.at[n], recv.at[r, k], peer(r, k)[2]) for n, (r, k) in enumerate(peers)]
    for copy in copies:
        copy.start()
    o_ref[2 * c + y, z] = x_ref[...]
    for n, (r, k) in enumerate(peers):
        pz, pq, dev = peer(r, 4 - k)
        remote(x_ref, o_ref.at[pq, pz], send.at[n], recv.at[r, k], dev).wait_recv()
    for copy in copies:
        copy.wait_send()


def small_gather(x, cid):
    return pl.pallas_call(
        small_gather_body, out_shape=jax.ShapeDtypeStruct((4, 4) + x.shape, x.dtype),
        in_specs=[pl.BlockSpec(memory_space=pltpu.VMEM)], out_specs=pl.BlockSpec(memory_space=pltpu.VMEM),
        scratch_shapes=[pltpu.SemaphoreType.DMA((15,)), pltpu.SemaphoreType.DMA((4, 4))],
        compiler_params=pltpu.CompilerParams(collective_id=cid, has_side_effects=True))(x)


def row_gather_body(x_ref, o_ref, up_s, dn_s, y_s, c_s, recv):
    z, y, c = place()
    barrier = pltpu.get_barrier_semaphore()
    me = tp_of(z, y, c)
    y_dev, c_dev = tp_of(z, 1 - y, c), tp_of(z, y, 1 - c)
    has_up, has_dn = z < 3, z > 0

    def greet(dev):
        pl.semaphore_signal(barrier, inc=1, device_id={'tp': dev}, device_id_type=MESH)

    greet(y_dev)
    greet(c_dev)
    pl.when(has_up)(lambda: greet(me + 4))
    pl.when(has_dn)(lambda: greet(me - 4))
    pl.semaphore_wait(barrier, 2 + has_up.astype(jnp.int32) + has_dn.astype(jnp.int32))

    q, qy = 2 * c + y, 2 * c + 1 - y
    quarter = [q, qy, 2 * (1 - c) + y, 2 * (1 - c) + 1 - y]

    def up(src, b):
        return remote(src, o_ref.at[q, b], up_s.at[b], recv.at[0, b], me + 4)

    def dn(src, b):
        return remote(src, o_ref.at[q, b], dn_s.at[b], recv.at[0, b], me - 4)

    def ycopy(src, b):
        return remote(src, o_ref.at[q, b], y_s.at[b], recv.at[1, b], y_dev)

    def ccopy(src, r, b):
        return remote(src, o_ref.at[quarter[r], b], c_s.at[r, b], recv.at[r + 2, b], c_dev)

    def landed(r, b):
        remote(x_ref, o_ref.at[quarter[r], b], c_s.at[0, b], recv.at[r, b], c_dev).wait_recv()

    pl.when(has_up)(lambda: up(x_ref, z).start())
    pl.when(has_dn)(lambda: dn(x_ref, z).start())
    ycopy(x_ref, z).start()
    ccopy(x_ref, 0, z).start()
    o_ref[q, z] = x_ref[...]
    for k in (1, 2, 3):
        lo, hi = z - k, z + k

        @pl.when(lo >= 0)
        def _():
            landed(0, lo)
            pl.when(has_up)(lambda: up(o_ref.at[q, lo], lo).start())
            ycopy(o_ref.at[q, lo], lo).start()
            ccopy(o_ref.at[q, lo], 0, lo).start()

        @pl.when(hi <= 3)
        def _():
            landed(0, hi)
            pl.when(has_dn)(lambda: dn(o_ref.at[q, hi], hi).start())
            ycopy(o_ref.at[q, hi], hi).start()
            ccopy(o_ref.at[q, hi], 0, hi).start()
    for k in range(4):
        for b, ok in ((z - k, z - k >= 0), (z + k, z + k <= 3)) if k else ((z, z >= 0),):
            @pl.when(ok)
            def _():
                landed(1, b)
                ccopy(o_ref.at[qy, b], 1, b).start()
    for b in range(4):
        landed(2, b)
        landed(3, b)
    for b in range(4):
        pl.when(has_up & (z >= b))(lambda: up(o_ref.at[q, b], b).wait_send())
        pl.when(has_dn & (z <= b))(lambda: dn(o_ref.at[q, b], b).wait_send())
        ycopy(o_ref.at[q, b], b).wait_send()
        ccopy(o_ref.at[q, b], 0, b).wait_send()
        ccopy(o_ref.at[qy, b], 1, b).wait_send()


def row_gather(x, cid):
    return pl.pallas_call(
        row_gather_body, out_shape=jax.ShapeDtypeStruct((4, 4) + x.shape, x.dtype),
        in_specs=[pl.BlockSpec(memory_space=pltpu.VMEM)], out_specs=pl.BlockSpec(memory_space=pltpu.VMEM),
        scratch_shapes=[pltpu.SemaphoreType.DMA((4,)), pltpu.SemaphoreType.DMA((4,)), pltpu.SemaphoreType.DMA((4,)),
                        pltpu.SemaphoreType.DMA((2, 4)), pltpu.SemaphoreType.DMA((4, 4))],
        compiler_params=pltpu.CompilerParams(collective_id=cid, has_side_effects=True, vmem_limit_bytes=16 * 1024 * 1024),
        cost_estimate=pl.CostEstimate(flops=30_000_000_000, bytes_accessed=2 * 16 * x.size, transcendentals=0))(x)


def logits_body(chunk, x_ref, e_ref, t_ref, z_ref, s_ref):
    tm = x_ref.shape[0]
    vocab = e_ref.shape[0]
    x = x_ref[...]
    tgt = t_ref[...].T[:, 0:1].astype(jnp.int32)
    m = s = t = None
    lane = lax.broadcasted_iota(jnp.int32, (tm, 128), 1)
    for j in range(vocab // chunk):
        z = lax.dot_general(x, e_ref[pl.ds(j * chunk, chunk), :], (((1,), (1,)), ((), ())), preferred_element_type=F32)
        z_ref[:, pl.ds(j * chunk, chunk)] = z
        parts = [z[:, k * 128:(k + 1) * 128] for k in range(chunk // 128)]
        hits = [jnp.where(lane == tgt - (j * chunk + k * 128), p, 0.0) for k, p in enumerate(parts)]
        n = functools.reduce(jnp.maximum, parts if m is None else [m] + parts)
        add = functools.reduce(jnp.add, [jnp.exp(p - n) for p in parts])
        s = add if m is None else s * jnp.exp(m - n) + add
        t = functools.reduce(jnp.add, hits if t is None else [t] + hits)
        m = n
    mx = jnp.max(m, axis=1, keepdims=True)
    sm = jnp.sum(s * jnp.exp(m - mx), axis=1, keepdims=True)
    tt = jnp.sum(t, axis=1, keepdims=True)
    s_ref[...] = jnp.where(lane == 0, mx, jnp.where(lane == 1, sm, tt)).T[:8, :]


def logits_call(x, e, rows8):
    b, d = x.shape
    v = e.shape[0]
    tm = 256
    return pl.pallas_call(
        functools.partial(logits_body, 512), grid=(b // tm,),
        in_specs=[pl.BlockSpec((tm, d), lambda i: (i, 0)),
                  pl.BlockSpec((v, d), lambda i: (0, 0), pipeline_mode=pl.Buffered(1)),
                  pl.BlockSpec((8, tm), lambda i: (0, i))],
        out_specs=[pl.BlockSpec((tm, v), lambda i: (i, 0)), pl.BlockSpec((8, tm), lambda i: (0, i))],
        out_shape=[jax.ShapeDtypeStruct((b, v), F32), jax.ShapeDtypeStruct((8, b), F32)],
        compiler_params=pltpu.CompilerParams(vmem_limit_bytes=VMEM_LIMIT),
        cost_estimate=pl.CostEstimate(flops=2 * b * d * v, bytes_accessed=4 * b * v, transcendentals=b * v))(x, e, rows8)


def grad_body(sub, nb, perm, z_ref, e_ref, r_ref, dz_ref, c_ref, y_ref, o_ref):
    tm, v = z_ref.shape
    i = pl.program_id(0)
    cols = r_ref[...].T
    res = []
    for a in range(tm // sub):
        r = pl.ds(a * sub, sub)
        lse, w, tgt = [cols[a * sub:(a + 1) * sub, k:k + 1] for k in range(3)]
        p = jnp.exp(z_ref[r, :] - lse)
        lane = lax.broadcasted_iota(jnp.int32, (sub, v), 1)
        p = jnp.where(lane == tgt.astype(jnp.int32), p - 1.0, p)
        dz = (p * w).astype(BF)
        dz_ref[r, :] = dz
        res.append(jnp.dot(dz, e_ref[...], preferred_element_type=F32))

    def put(ref):
        for a, val in enumerate(res):
            ref[pl.ds(a * sub, sub), :] = val

    pl.when(i < 2 * nb)(lambda: put(c_ref))
    pl.when((i >= 2 * nb) & (i < 3 * nb))(lambda: put(y_ref))
    pl.when(i >= 3 * nb)(lambda: put(o_ref))


def grad_call(z, e, rows8, perm):
    b, v = z.shape
    d = e.shape[1]
    tm = TM_GRAD
    nb = b // 4 // tm
    row = lambda i, p: (p[lax.div(i, nb)] * nb + lax.rem(i, nb), 0)
    return pl.pallas_call(
        functools.partial(grad_body, 128, nb),
        grid_spec=pltpu.PrefetchScalarGridSpec(
            num_scalar_prefetch=1, grid=(b // tm,),
            in_specs=[pl.BlockSpec((tm, v), row),
                      pl.BlockSpec((v, d), lambda i, p: (0, 0), pipeline_mode=pl.Buffered(1)),
                      pl.BlockSpec((8, tm), lambda i, p: row(i, p)[::-1])],
            out_specs=[pl.BlockSpec((tm, v), row),
                       pl.BlockSpec((tm, d), lambda i, p: (jnp.minimum(i, 2 * nb - 1), 0)),
                       pl.BlockSpec((tm, d), lambda i, p: (jnp.clip(i - 2 * nb, 0, nb - 1), 0)),
                       pl.BlockSpec((tm, d), lambda i, p: (jnp.clip(i - 3 * nb, 0, nb - 1), 0))]),
        out_shape=[jax.ShapeDtypeStruct((b, v), BF), jax.ShapeDtypeStruct((b // 2, d), F32),
                   jax.ShapeDtypeStruct((b // 4, d), F32), jax.ShapeDtypeStruct((b // 4, d), F32)],
        compiler_params=pltpu.CompilerParams(vmem_limit_bytes=VMEM_LIMIT),
        cost_estimate=pl.CostEstimate(flops=2 * b * d * v, bytes_accessed=6 * b * v,
                                      transcendentals=b * v))(perm, z, e, rows8)


TN = (((0,), (0,)), ((), ()))


def embed_body(a_ref, b_ref, xa_ref, xb_ref, o_ref):
    o_ref[...] = lax.dot_general(a_ref[...], xa_ref[...], TN, preferred_element_type=F32)
    o_ref[...] += lax.dot_general(b_ref[...], xb_ref[...], TN, preferred_element_type=F32)


def embed_call(da, db, xa, xb):
    b, v = da.shape
    d = xa.shape[1]
    tv = 256
    col = pl.BlockSpec((b, tv), lambda j: (0, j))
    full = pl.BlockSpec((b, d), lambda j: (0, 0), pipeline_mode=pl.Buffered(1))
    return pl.pallas_call(
        embed_body, grid=(v // tv,), in_specs=[col, col, full, full],
        out_specs=pl.BlockSpec((tv, d), lambda j: (j, 0)), out_shape=jax.ShapeDtypeStruct((v, d), F32),
        compiler_params=pltpu.CompilerParams(vmem_limit_bytes=VMEM_LIMIT),
        cost_estimate=pl.CostEstimate(flops=4 * b * d * v, bytes_accessed=4 * b * v, transcendentals=0))(da, db, xa, xb)


def weight_body(h_ref, g_ref, o_ref):
    o_ref[...] = lax.dot_general(h_ref[...], g_ref[...], TN, preferred_element_type=F32)


def weight_call(h, g):
    t, d = h.shape
    tv = 256
    return pl.pallas_call(
        weight_body, grid=(d // tv,),
        in_specs=[pl.BlockSpec((t, tv), lambda j: (0, j)),
                  pl.BlockSpec((t, d), lambda j: (0, 0), pipeline_mode=pl.Buffered(1))],
        out_specs=pl.BlockSpec((tv, d), lambda j: (j, 0)), out_shape=jax.ShapeDtypeStruct((d, d), F32),
        compiler_params=pltpu.CompilerParams(vmem_limit_bytes=VMEM_LIMIT),
        cost_estimate=pl.CostEstimate(flops=2 * t * d * d, bytes_accessed=4 * d * d, transcendentals=0))(h, g)


def layer_norm(values, gain, bias):
    mean_val = jnp.mean(values, axis=-1, keepdims=True)
    centered = values - mean_val
    variance = jnp.mean(centered * centered, axis=-1, keepdims=True)
    return centered * lax.rsqrt(variance + LN_EPS) * gain + bias


def norm_back_body(p0, p1, p2, p3, a_ref, g_ref, da_ref, db_ref, s_ref):
    dy = (p0[...] + p1[...]) + (p2[...] + p3[...])
    a = a_ref[...].astype(F32)
    cen = a - jnp.mean(a, axis=1, keepdims=True)
    inv = lax.rsqrt(jnp.mean(cen * cen, axis=1, keepdims=True) + LN_EPS)
    hat = cen * inv
    dh = dy * g_ref[...]
    da = inv * (dh - jnp.mean(dh, axis=1, keepdims=True) - hat * jnp.mean(dh * hat, axis=1, keepdims=True))
    da_ref[...] = da
    db_ref[...] = da.astype(BF)
    ds = jnp.sum(dy * hat, axis=0, keepdims=True)
    dt = jnp.sum(dy, axis=0, keepdims=True)
    row = lax.broadcasted_iota(jnp.int32, s_ref.shape, 0)
    s_ref[...] = jnp.where(row == 0, ds, jnp.where(row == 1, dt, 0.0))


def norm_back(parts, a, gain):
    t, d = a.shape
    vm = pl.BlockSpec(memory_space=pltpu.VMEM)
    return pl.pallas_call(
        norm_back_body, in_specs=[vm] * 6, out_specs=[vm] * 3,
        out_shape=[jax.ShapeDtypeStruct((t, d), F32), jax.ShapeDtypeStruct((t, d), BF), jax.ShapeDtypeStruct((8, d), F32)],
        compiler_params=pltpu.CompilerParams(vmem_limit_bytes=24 * 1024 * 1024),
        cost_estimate=pl.CostEstimate(flops=1_000_000_000, bytes_accessed=22 * t * d, transcendentals=t))(*parts, a, gain)


TM_GRAD = 256


def solution(mesh):
    tok_spec = P(('dp', 'tp'), None)
    row_spec = P(None, ('dp', 'tp'))

    def step(hidden, w_two, ln_scale, ln_shift, embed, targets, loss_mask):
        toks, width = hidden.shape
        shard_rows = embed.shape[0]
        zi, yi, ci = place()
        base = (lax.axis_index('tp') * shard_rows).astype(F32)
        mine = 2 * ci + yi
        perm = jnp.stack([3 - mine, 2 * (1 - ci) + yi, 2 * ci + 1 - yi, mine])
        ints = small_gather(jnp.concatenate([targets, loss_mask, jnp.zeros((4, toks), jnp.int32)], axis=0), 1)
        h_all = row_gather(hidden, 2).reshape(16 * toks, width)
        mask = [ints[:, :, 2 + h].astype(F32).reshape(-1) for h in range(2)]
        count = [jnp.sum(m) for m in mask]

        def forward(h, a, cid):
            x = layer_norm(a.astype(F32), ln_scale[h], ln_shift[h]).astype(BF)
            tgt = ints[:, :, h].reshape(-1).astype(F32) - base
            z, st = logits_call(x, embed, jnp.broadcast_to(tgt, (8, tgt.shape[0])))
            part = jnp.concatenate([(st[0] + jnp.log(st[1])).reshape(-1, 128), st[2].reshape(-1, 128)], axis=0)
            parts = small_gather(part, cid).reshape(16, 2, -1, 128)
            top = jnp.max(parts[:, 0], axis=0)
            lse = top + jnp.log(jnp.sum(jnp.exp(parts[:, 0] - top), axis=0))
            raw = (lse - jnp.sum(parts[:, 1], axis=0)).reshape(-1)
            wgt = mask[h] / count[h]
            rows8 = jnp.concatenate([jnp.stack([lse.reshape(-1), wgt, tgt]), jnp.zeros((5, tgt.shape[0]), F32)], axis=0)
            dz, to_core, to_y, own = grad_call(z, embed, rows8, perm)
            loss = raw * mask[h]
            own_loss = lax.dynamic_slice_in_dim(loss, (mine * 4 + zi) * toks, toks)
            return x, dz, (to_core, to_y, own), own_loss, jnp.sum(loss / count[h])

        def exchange(to_core, to_y, own):
            n = own.shape[0]
            from_core = lax.ppermute(to_core, 'tp', CORE_PAIRS)
            halves = []
            for k in range(2):
                rows = slice(k * n // 2, (k + 1) * n // 2)
                send = to_y[rows] + from_core[:n][rows]
                halves.append(own[rows] + from_core[n:][rows] + lax.ppermute(send, 'tp', Y_PAIRS))
            part = jnp.concatenate(halves, axis=0).reshape(4, toks, width)
            parts = [lax.dynamic_index_in_dim(part, zi, 0, keepdims=False)]
            for k in (1, 2, 3):
                block = lax.dynamic_index_in_dim(part, lax.rem(zi + k, 4), 0, keepdims=False)
                parts.append(lax.ppermute(block, 'tp', Z_PAIRS[k]))
            return parts

        a_all = jnp.dot(h_all, w_two, preferred_element_type=F32).astype(BF)
        x_b, dz_b, send_b, loss_b, tot_b = forward(1, a_all, 3)
        dx_b = exchange(*send_b)
        h_one, _ = lax.optimization_barrier((h_all, send_b[2]))
        x_a, dz_a, send_a, loss_a, tot_a = forward(0, h_one, 4)
        dx_a = exchange(*send_a)
        d_embed = embed_call(dz_a, dz_b, x_a, x_b)

        proj_loc = jnp.dot(hidden, w_two, preferred_element_type=F32).astype(BF)
        _, d_proj, sums_b = norm_back(dx_b, proj_loc, ln_scale[1:2])
        g_all = row_gather(d_proj, 5).reshape(16 * toks, width)
        d_w_two = weight_call(h_all, g_all)
        via_two = lax.dot_general(d_proj, w_two, (((1,), (1,)), ((), ())), preferred_element_type=F32)
        da_a, _, sums_a = norm_back(dx_a, hidden, ln_scale[0:1])
        d_hidden = (da_a + via_two).astype(BF)
        ln_part = jnp.concatenate([v.reshape(-1, 128) for v in (sums_a[0], sums_b[0], sums_a[1], sums_b[1])], axis=0)
        ln_all = jnp.sum(small_gather(ln_part, 6).reshape(16, 4, width), axis=0)
        token_loss = jnp.stack([loss_a, loss_b])
        return token_loss, (tot_a + tot_b).reshape(1), d_hidden, d_embed, d_w_two, ln_all[:2], ln_all[2:]

    return jax.shard_map(step, mesh=mesh,
                         in_specs=(tok_spec, P(), P(), P(), P('tp', None), row_spec, row_spec),
                         out_specs=(row_spec, P('dp'), tok_spec, tok_spec, P('dp', None), P('dp', None), P('dp', None)),
                         check_vma=False)
```

time: 1080 us -> 707 us (0.65)
  Pallas kernels: 0 us -> 488 us
  waiting for transfers between devices: 576 us -> 92.1 us
  matrix products: 229 us -> 26.2 us
  blocking collectives: 201 us -> 0 us
  other arithmetic: 35.1 us -> 66.3 us
  local copies, waits for them, and re-layouts: 22 us -> 8.69 us
  starting transfers between devices: 0.34 us -> 12.9 us
    pallas_call x0 -> x14, Pallas kernels: none -> 488 us  [the longest x2 191 us: row_gather(): pl.pallas_call(row_gather_body, out_shape=jax.ShapeDtypeStruct((4, 4) + x...]
    reduce_scatter x1 -> x0, waiting for transfers between devices: 324 us -> none  [device_step(): dx_loc = lax.psum_scatter(dx_part, 'tp', scatter_dimension=1, tiled=True)]
    dot_general x6 -> x3, matrix products: 229 us -> 26.2 us  [the longest x1 18.3 us: step(): a_all = jnp.dot(h_all, w_two, preferred_element_type=F32).astype(BF)]
    psum x1 -> x0, waiting for transfers between devices: 148 us -> none  [device_step(): lax.psum((d_w_part, d_scale_part, d_shift_part), 'tp')]
    psum x2 -> x0, blocking collectives: 119 us -> none  [the longest x1 61.2 us: device_step(): lax.psum((d_w_part, d_scale_part, d_shift_part), 'tp')]
    all_gather x1 -> x0, waiting for transfers between devices: 103 us -> none  [device_step(): x_all = lax.all_gather(x_loc, 'tp', axis=1, tiled=True)]
    ppermute x0 -> x12, waiting for transfers between devices: none -> 92.1 us  [the longest x4 92 us: exchange(): lax.ppermute(send, 'tp', Y_PAIRS)]
    pmax x1 -> x0, blocking collectives: 59.3 us -> none  [device_step(): glob_max = lax.pmax(local_max, 'tp')]
  transfers between devices with their start and end apart: 3 -> 12, of which waited for: 3 -> 3; matrix products, arithmetic and copies ran while one was open for 9% -> 8% of each run, Pallas kernels for 0% -> 42%
where the time goes in v1:
time: 707 us; the launch traced here: 698 us
  Pallas kernels  488 us (69%)
  waiting for transfers between devices  92.1 us (13%)
  other arithmetic  66.3 us (9%)
  matrix products  26.2 us (4%)
  starting transfers between devices  12.9 us (2%)
  local copies, waits for them, and re-layouts  8.69 us (1%)
    pallas_call x2, Pallas kernels, row_gather(): pl.pallas_call(row_gather_body, out_shape=jax.ShapeDtypeStruct((4, 4) + x...  191 us
    ppermute x4, waiting for transfers between devices, exchange(): lax.ppermute(send, 'tp', Y_PAIRS)  92 us
    pallas_call x2, Pallas kernels, grad_call(): pl.pallas_call(functools.partial(grad_body, 128, nb), grid_spec=pltpu.Pre...  85 us
    pallas_call x2, Pallas kernels, logits_call(): pl.pallas_call(functools.partial(logits_body, 512), grid=(b // tm,), in_s...  75 us
    pallas_call x1, Pallas kernels, embed_call(): pl.pallas_call(embed_body, grid=(v // tv,), in_specs=[col, col, full, ful...  62.5 us
    pallas_call x4, Pallas kernels, small_gather(): pl.pallas_call(small_gather_body, out_shape=jax.ShapeDtypeStruct((4, 4) +...  46.4 us
    pallas_call x1, Pallas kernels, weight_call(): pl.pallas_call(weight_body, grid=(d // tv,), in_specs=[pl.BlockSpec((t, t...  24 us
    dot_general x1, matrix products, step(): a_all = jnp.dot(h_all, w_two, preferred_element_type=F32).astype(BF)  18.3 us
  transfers between devices with their start and end apart: 12, of which 3 were waited for; matrix products, arithmetic and copies ran while one was open for 8% of the time, Pallas kernels for 42%

profile of v1, /device:TPU:0, one launch (start us, length us, event | category | flops | bytes accessed | tf_op | source)
XLA Modules:
  0.0 698.1 jit_solution(456302836751489905)
XLA Ops:
  0.7 1.0 copy-done.1
  1.7 55.0 %shard_map.126 = bf16[4,4,128,2048]{3,2,1,0:T(8,128)(2,1)S(1)} custom-call(bf16[128,2048]{1,0:T(8,128)(2,1)S(1)} %copy-done.1), custom_call_target="tpu_custom_call" | custom-call | flops 30000001024 | bytes 8388608 | tf_op jit(solution)/shard_map/pallas_call | solution.py:142
  56.7 18.3 %convert_reduce_fusion.1 = (f32[2048]{0:T(1024)S(1)}, bf16[2048,2048]{1,0:T(8,128)(2,1)S(1)}) fusion(bf16[2048,2048]{1,0:T(8,128)(2,1)S(1)} %bitcast.75, bf16[2048,2048]{1,0:T(8,128)(2,1)S(1)} %copy-done.8), kind=kOutput, calls=%fused_computation.3 | convolution fusion | flops 17192450048 | bytes 25174016 | tf_op jit(solution)/shard_map/dot_general | solution.py:357
  75.1 2.3 fusion.8
  77.4 1.0 copy-done.9
  79.3 8.1 %shard_map.127 = s32[4,4,8,128]{3,2,1,0:T(8,128)} custom-call(s32[8,128]{1,0:T(8,128)} %add_add_fusion.x_ref), custom_call_target="tpu_custom_call" | custom-call | tf_op jit(solution)/shard_map/pallas_call | solution.py:62
  87.3 1.6 fusion.25
  88.9 8.7 %fusion.11.x_ref.xb_ref = bf16[2048,2048]{1,0:T(8,128)(2,1)} fusion(bf16[2048,2048]{1,0:T(8,128)(2,1)} %copy-done.9, f32[2048]{0:T(1024)S(1)} %bitcast.102, f32[2048]{0:T(1024)S(1)} %bitcast.83, f32[2048]{0:T(1024)S(1)} %add_rsqrt_fusion.1, f32[2048]{0:T(1024)S(1)} %broadcast_multiply_fusion.1), kind=kLoop, calls=%fused_computation.15 | loop fusion | flops 25165824 | bytes 16809984 | tf_op jit(solution)/shard_map/convert_element_type | solution.py:327
  97.6 1.3 broadcast_divide_fusion
  99.6 37.4 %shard_map.128 = (f32[2048,3072]{1,0:T(8,128)}, f32[8,2048]{1,0:T(8,128)}) custom-call(bf16[2048,2048]{1,0:T(8,128)(2,1)} %fusion.11.x_ref.xb_ref, bf16[3072,2048]{1,0:T(8,128)(2,1)} %e_ref.7, f32[8,2048]{1,0:T(8,128)} %broadcast_in_dim.7.t_ref), custom_call_target="tpu_custom_call" | custom-call | flops 25769803776 | bytes 25165824 | tf_op jit(solution)/shard_map/pallas_call | solution.py:178
  136.9 1.0 log_add_fusion.3
  138.5 10.9 %shard_map.129 = f32[4,4,32,128]{3,2,1,0:T(8,128)} custom-call(f32[32,128]{1,0:T(8,128)} %pad_maximum_fusion.3.x_ref), custom_call_target="tpu_custom_call" | custom-call | tf_op jit(solution)/shard_map/pallas_call | solution.py:62
  149.4 1.0 slice_reduce_fusion
  150.4 0.9 fusion.19
  152.8 42.2 %shard_map.130 = (bf16[2048,3072]{1,0:T(8,128)(2,1)}, f32[1024,2048]{1,0:T(8,128)}, f32[512,2048]{1,0:T(8,128)}, f32[512,2048]{1,0:T(8,128)}) custom-call(s32[4]{0:T(128)} %pad_add_fusion.perm, f32[2048,3072]{1,0:T(8,128)} %get-tuple-element.24.z_ref, bf16[3072,2048]{1,0:T(8,128)(2,1)} %e_ref.7, f32[8,2048]{1,0:T(8,128)} %maximum_maximum_fusion.r_ref), custom_call_target="tpu_custom_call" | custom-call | flops 25769803776 | bytes 37748736 | tf_op jit(solution)/shard_map/pallas_call | solution.py:219
  195.0 0.9 collective-permute-start.6
  196.0 4.7 convert_reduce_fusion
  200.7 5.8 fusion.4
  206.6 5.5 fusion.7.x_ref.xa_ref
  212.7 37.6 %shard_map.131 = (f32[2048,3072]{1,0:T(8,128)}, f32[8,2048]{1,0:T(8,128)}) custom-call(bf16[2048,2048]{1,0:T(8,128)(2,1)} %fusion.7.x_ref.xa_ref, bf16[3072,2048]{1,0:T(8,128)(2,1)} %e_ref.7, f32[8,2048]{1,0:T(8,128)} %broadcast_in_dim.8.t_ref), custom_call_target="tpu_custom_call" | custom-call | flops 25769803776 | bytes 25165824 | tf_op jit(solution)/shard_map/pallas_call | solution.py:178
  250.3 1.0 log_add_fusion.1
  251.8 10.9 %shard_map.132 = f32[4,4,32,128]{3,2,1,0:T(8,128)} custom-call(f32[32,128]{1,0:T(8,128)} %pad_maximum_fusion.4.x_ref), custom_call_target="tpu_custom_call" | custom-call | tf_op jit(solution)/shard_map/pallas_call | solution.py:62
  262.7 1.0 slice_reduce_fusion.1
  263.7 0.9 fusion.17
  265.4 42.8 %shard_map.133 = (bf16[2048,3072]{1,0:T(8,128)(2,1)}, f32[1024,2048]{1,0:T(8,128)}, f32[512,2048]{1,0:T(8,128)}, f32[512,2048]{1,0:T(8,128)}) custom-call(s32[4]{0:T(128)} %pad_add_fusion.perm, f32[2048,3072]{1,0:T(8,128)} %get-tuple-element.29.z_ref, bf16[3072,2048]{1,0:T(8,128)(2,1)} %e_ref.7, f32[8,2048]{1,0:T(8,128)} %maximum_maximum_fusion.1.r_ref), custom_call_target="tpu_custom_call" | custom-call | flops 25769803776 | bytes 37748736 | tf_op jit(solution)/shard_map/pallas_call | solution.py:219
  309.1 4.5 slice_add_fusion.2
  314.2 1.4 collective-permute-start.8
  315.6 62.5 %shard_map.136 = f32[3072,2048]{1,0:T(8,128)} custom-call(bf16[2048,3072]{1,0:T(8,128)(2,1)} %get-tuple-element.37.a_ref, bf16[2048,3072]{1,0:T(8,128)(2,1)} %get-tuple-element.38.b_ref, bf16[2048,2048]{1,0:T(8,128)(2,1)} %fusion.7.x_ref.xa_ref, bf16[2048,2048]{1,0:T(8,128)(2,1)} %fusion.11.x_ref.xb_ref), custom_call_target="tpu_custom_call" | custom-call | flops 51539607552 | bytes 25165824 | tf_op jit(solution)/shard_map/pallas_call | solution.py:251
  378.1 2.0 fusion.21
  380.1 6.6 slice_add_fusion.6
  387.2 1.4 collective-permute-start.2
  390.6 4.9 convolution_convert_fusion.1.a_ref
  395.5 11.8 %collective-permute-done.8 = f32[256,2048]{1,0:T(8,128)} collective-permute-done((f32[256,2048]{1,0:T(8,128)S(1)}, f32[256,2048]{1,0:T(8,128)}, u32[]{:S(2)}, u32[]{:S(2)}) %collective-permute-start.8) | collective-permute-done | bytes 2097184 | tf_op jit(solution)/shard_map/ppermute | solution.py:349
  407.3 4.9 fusion.13
  413.6 2.4 collective-permute-start.11
  415.9 36.3 %collective-permute-done.1 = f32[256,2048]{1,0:T(8,128)} collective-permute-done((f32[256,2048]{1,0:T(8,128)}, f32[256,2048]{1,0:T(8,128)}, u32[]{:S(2)}, u32[]{:S(2)}) %collective-permute-start.1) | collective-permute-done | bytes 2097184 | tf_op jit(solution)/shard_map/ppermute | solution.py:349
  452.2 44.0 %collective-permute-done.2 = f32[256,2048]{1,0:T(8,128)} collective-permute-done((f32[256,2048]{1,0:T(8,128)}, f32[256,2048]{1,0:T(8,128)}, u32[]{:S(2)}, u32[]{:S(2)}) %collective-permute-start.2) | collective-permute-done | bytes 2097184 | tf_op jit(solution)/shard_map/ppermute | solution.py:349
  496.2 4.9 fusion.15
  502.6 1.5 collective-permute-start.4
  504.2 1.5 collective-permute-start.5
  505.6 2.1 shard_map.135
  507.7 136.0 %shard_map.137 = bf16[4,4,128,2048]{3,2,1,0:T(8,128)(2,1)S(1)} custom-call(bf16[128,2048]{1,0:T(8,128)(2,1)S(1)} %get-tuple-element.36.x_ref), custom_call_target="tpu_custom_call" | custom-call | flops 30000001024 | bytes 8388608 | tf_op jit(solution)/shard_map/pallas_call | solution.py:142
  643.7 3.2 copy-done.7
  647.0 2.9 fusion.33
  649.9 1.9 shard_map.134
  652.5 16.7 %shard_map.139 = f32[4,4,64,128]{3,2,1,0:T(8,128)} custom-call(f32[64,128]{1,0:T(8,128)} %pad_maximum_fusion.2.x_ref), custom_call_target="tpu_custom_call" | custom-call | tf_op jit(solution)/shard_map/pallas_call | solution.py:62
  669.2 1.1 reduce_sum.129
  671.5 24.0 %shard_map.138 = f32[2048,2048]{1,0:T(8,128)} custom-call(bf16[2048,2048]{1,0:T(8,128)(2,1)} %bitcast.78, bf16[2048,2048]{1,0:T(8,128)(2,1)} %bitcast.84), custom_call_target="tpu_custom_call" | custom-call | flops 17179869184 | bytes 16777216 | tf_op jit(solution)/shard_map/pallas_call | solution.py:265
  (94 shorter events, 14.0 us)
Async XLA Ops:
  0.6 1.0 copy-start.1
  1.7 55.0 %copy-start.8 = (bf16[2048,2048]{1,0:T(8,128)(2,1)S(1)}, bf16[2048,2048]{1,0:T(8,128)(2,1)}, u32[]{:S(2)}) copy-start(bf16[2048,2048]{1,0:T(8,128)(2,1)} %param.8) | copy-start | bytes 25165828
  56.7 18.4 %copy-start = (bf16[4,4,128,2048]{3,2,1,0:T(8,128)(2,1)}, bf16[4,4,128,2048]{3,2,1,0:T(8,128)(2,1)S(1)}, u32[]{:S(2)}) copy-start(bf16[4,4,128,2048]{3,2,1,0:T(8,128)(2,1)S(1)} %shard_map.126) | copy-start | bytes 25165828
  75.0 3.4 copy-start.9
  75.1 3.4 copy-start.15
  75.1 3.4 copy-start.16
  75.1 3.5 copy-start.17
  75.1 3.5 copy-start.18
  78.5 19.1 %copy-start.5 = (f32[1,2048]{1,0:T(1,128)}, f32[1,2048]{1,0:T(1,128)S(1)}, u32[]{:S(2)}) copy-start(f32[1,2048]{1,0:T(1,128)S(1)} %get-tuple-element.86.g_ref) | copy-start | bytes 24580
  78.5 128.0 %copy-start.3 = (f32[1,2048]{1,0:T(1,128)}, f32[1,2048]{1,0:T(1,128)S(1)}, u32[]{:S(2)}) copy-start(f32[1,2048]{1,0:T(1,128)S(1)} %get-tuple-element.85.g_ref) | copy-start | bytes 24580
  88.9 8.7 %copy-start.13 = (s32[4,4,8,128]{3,2,1,0:T(8,128)S(1)}, s32[4,4,8,128]{3,2,1,0:T(8,128)}, u32[]{:S(2)}) copy-start(s32[4,4,8,128]{3,2,1,0:T(8,128)} %shard_map.127) | copy-start | bytes 196612
  195.0 114.0 %collective-permute-start.6 = (f32[1024,2048]{1,0:T(8,128)}, f32[1024,2048]{1,0:T(8,128)}, u32[]{:S(2)}, u32[]{:S(2)}) collective-permute-start(f32[1024,2048]{1,0:T(8,128)} %get-tuple-element.34), channel_id=1, source_target_pairs={{0,1},{1,0},{2,3},{3,2},{4,5},{5,4},{6,7},{7,6},{8,9},{9,8},{10,11... | collective-permute-start | bytes 25165832 | tf_op jit(solution)/shard_map/ppermute | solution.py:344
  196.0 10.6 %slice-start = ((s8[8388608]{0:T(1024)(128)(4,1)}), s8[4194304]{0:T(1024)(128)(4,1)S(1)}, s32[]{:S(2)}) async-start(s8[8388608]{0:T(1024)(128)(4,1)} %bitcast.79), calls=%async_computation | async-start | bytes 8388608
  200.7 5.9 slice-start.1
  265.4 43.7 %copy-start.10 = (f32[512,2048]{1,0:T(8,128)S(1)}, f32[512,2048]{1,0:T(8,128)}, u32[]{:S(2)}) copy-start(f32[512,2048]{1,0:T(8,128)} %get-tuple-element.35) | copy-start | bytes 12582916
  308.1 71.9 %collective-permute-start = (f32[1024,2048]{1,0:T(8,128)}, f32[1024,2048]{1,0:T(8,128)}, u32[]{:S(2)}, u32[]{:S(2)}) collective-permute-start(f32[1024,2048]{1,0:T(8,128)} %get-tuple-element.31), channel_id=1, source_target_pairs={{0,1},{1,0},{2,3},{3,2},{4,5},{5,4},{6,7},{7,6},{8,9},{9,8},{10,11... | collective-permute-start | bytes 25165832 | tf_op jit(solution)/shard_map/ppermute | solution.py:344
  313.5 82.0 %collective-permute-start.7 = (f32[256,2048]{1,0:T(8,128)}, f32[256,2048]{1,0:T(8,128)}, u32[]{:S(2)}, u32[]{:S(2)}) collective-permute-start(f32[256,2048]{1,0:T(8,128)} %get-tuple-element.55), channel_id=1, source_target_pairs={{0,2},{1,3},{2,0},{3,1},{4,6},{5,7},{6,4},{7,5},{8,10},{9,11},{10,... | collective-permute-start | bytes 6291464 | tf_op jit(solution)/shard_map/ppermute | solution.py:349
  314.2 93.1 %collective-permute-start.8 = (f32[256,2048]{1,0:T(8,128)S(1)}, f32[256,2048]{1,0:T(8,128)}, u32[]{:S(2)}, u32[]{:S(2)}) collective-permute-start(f32[256,2048]{1,0:T(8,128)S(1)} %get-tuple-element.56), channel_id=1, source_target_pairs={{0,2},{1,3},{2,0},{3,1},{4,6},{5,7},{6,4},{7,5},{8,10},{9,11},{10,... | collective-permute-start | bytes 6291464 | tf_op jit(solution)/shard_map/ppermute | solution.py:349
  315.6 62.5 %copy-start.14 = (s32[4,4,8,128]{3,2,1,0:T(8,128)S(1)}, s32[4,4,8,128]{3,2,1,0:T(8,128)}, u32[]{:S(2)}) copy-start(s32[4,4,8,128]{3,2,1,0:T(8,128)} %shard_map.127) | copy-start | bytes 196612
  378.1 12.5 %copy-start.2 = (bf16[128,2048]{1,0:T(8,128)(2,1)S(1)}, bf16[128,2048]{1,0:T(8,128)(2,1)}, u32[]{:S(2)}) copy-start(bf16[128,2048]{1,0:T(8,128)(2,1)} %a_ref.1) | copy-start | bytes 1572868
  386.6 65.6 %collective-permute-start.1 = (f32[256,2048]{1,0:T(8,128)}, f32[256,2048]{1,0:T(8,128)}, u32[]{:S(2)}, u32[]{:S(2)}) collective-permute-start(f32[256,2048]{1,0:T(8,128)} %get-tuple-element.59), channel_id=1, source_target_pairs={{0,2},{1,3},{2,0},{3,1},{4,6},{5,7},{6,4},{7,5},{8,10},{9,11},{10,... | collective-permute-start | bytes 6291464 | tf_op jit(solution)/shard_map/ppermute | solution.py:349
  387.2 109.0 %collective-permute-start.2 = (f32[256,2048]{1,0:T(8,128)}, f32[256,2048]{1,0:T(8,128)}, u32[]{:S(2)}, u32[]{:S(2)}) collective-permute-start(f32[256,2048]{1,0:T(8,128)} %get-tuple-element.60), channel_id=1, source_target_pairs={{0,2},{1,3},{2,0},{3,1},{4,6},{5,7},{6,4},{7,5},{8,10},{9,11},{10,... | collective-permute-start | bytes 6291464 | tf_op jit(solution)/shard_map/ppermute | solution.py:349
  390.0 17.3 %copy-start.11 = (f32[512,2048]{1,0:T(8,128)S(1)}, f32[512,2048]{1,0:T(8,128)}, u32[]{:S(2)}) copy-start(f32[512,2048]{1,0:T(8,128)} %get-tuple-element.26) | copy-start | bytes 12582916
  412.2 84.0 %copy-start.12 = (f32[512,2048]{1,0:T(8,128)S(1)}, f32[512,2048]{1,0:T(8,128)}, u32[]{:S(2)}) copy-start(f32[512,2048]{1,0:T(8,128)} %get-tuple-element.30) | copy-start | bytes 12582916
  412.8 91.4 %collective-permute-start.10 = (f32[128,2048]{1,0:T(8,128)S(1)}, f32[128,2048]{1,0:T(8,128)S(1)}, u32[]{:S(2)}, u32[]{:S(2)}) collective-permute-start(f32[128,2048]{1,0:T(8,128)S(1)} %get-tuple-element.62), channel_id=1, source_target_pairs={{0,8},{1,9},{2,10},{3,11},{4,12},{5,13},{6,14},{7,15},{8,0},{9,1},... | collective-permute-start | bytes 3145736 | tf_op jit(solution)/shard_map/ppermute | solution.py:354
  413.6 92.0 %collective-permute-start.11 = (f32[128,2048]{1,0:T(8,128)S(1)}, f32[128,2048]{1,0:T(8,128)S(1)}, u32[]{:S(2)}, u32[]{:S(2)}) collective-permute-start(f32[128,2048]{1,0:T(8,128)S(1)} %get-tuple-element.61), channel_id=1, source_target_pairs={{0,12},{1,13},{2,14},{3,15},{4,0},{5,1},{6,2},{7,3},{8,4},{9,5},{1... | collective-permute-start | bytes 3145736 | tf_op jit(solution)/shard_map/ppermute | solution.py:354
  415.9 89.7 %collective-permute-start.9 = (f32[128,2048]{1,0:T(8,128)S(1)}, f32[128,2048]{1,0:T(8,128)S(1)}, u32[]{:S(2)}, u32[]{:S(2)}) collective-permute-start(f32[128,2048]{1,0:T(8,128)S(1)} %get-tuple-element.63), channel_id=1, source_target_pairs={{0,4},{1,5},{2,6},{3,7},{4,8},{5,9},{6,10},{7,11},{8,12},{9,13},{1... | collective-permute-start | bytes 3145736 | tf_op jit(solution)/shard_map/ppermute | solution.py:354
  501.1 4.5 copy-start.6
  501.4 145.6 %slice-start.2 = ((s8[8388608]{0:T(1024)(128)(4,1)}), s8[4194304]{0:T(1024)(128)(4,1)S(1)}, s32[]{:S(2)}) async-start(s8[8388608]{0:T(1024)(128)(4,1)} %bitcast.85), calls=%async_computation.2 | async-start | bytes 8388608
  501.7 148.2 %collective-permute-start.3 = (f32[128,2048]{1,0:T(8,128)S(1)}, f32[128,2048]{1,0:T(8,128)S(1)}, u32[]{:S(2)}, u32[]{:S(2)}) collective-permute-start(f32[128,2048]{1,0:T(8,128)S(1)} %get-tuple-element.67), channel_id=1, source_target_pairs={{0,4},{1,5},{2,6},{3,7},{4,8},{5,9},{6,10},{7,11},{8,12},{9,13},{1... | collective-permute-start | bytes 3145736 | tf_op jit(solution)/shard_map/ppermute | solution.py:354
  502.6 147.3 %collective-permute-start.4 = (f32[128,2048]{1,0:T(8,128)S(1)}, f32[128,2048]{1,0:T(8,128)S(1)}, u32[]{:S(2)}, u32[]{:S(2)}) collective-permute-start(f32[128,2048]{1,0:T(8,128)S(1)} %get-tuple-element.66), channel_id=1, source_target_pairs={{0,8},{1,9},{2,10},{3,11},{4,12},{5,13},{6,14},{7,15},{8,0},{9,1},... | collective-permute-start | bytes 3145736 | tf_op jit(solution)/shard_map/ppermute | solution.py:354
  504.2 145.8 %collective-permute-start.5 = (f32[128,2048]{1,0:T(8,128)S(1)}, f32[128,2048]{1,0:T(8,128)S(1)}, u32[]{:S(2)}, u32[]{:S(2)}) collective-permute-start(f32[128,2048]{1,0:T(8,128)S(1)} %get-tuple-element.65), channel_id=1, source_target_pairs={{0,12},{1,13},{2,14},{3,15},{4,0},{5,1},{6,2},{7,3},{8,4},{9,5},{1... | collective-permute-start | bytes 3145736 | tf_op jit(solution)/shard_map/ppermute | solution.py:354
  507.7 139.3 %slice-start.3 = ((s8[8388608]{0:T(1024)(128)(4,1)}), s8[4194304]{0:T(1024)(128)(4,1)S(1)}, s32[]{:S(2)}) async-start(s8[8388608]{0:T(1024)(128)(4,1)} %bitcast.85), calls=%async_computation.3 | async-start | bytes 8388608
  643.7 3.3 copy-start.7
  647.0 3.0 copy-start.4

commit v2 on v0

v2 whole, which is shorter than its diff:
```python
import functools
import jax
import jax.numpy as jnp
from jax import lax
from jax.experimental import pallas as pl
from jax.experimental.pallas import tpu as pltpu
from jax.sharding import PartitionSpec as P

LN_EPS = 1e-5
F32 = jnp.float32
BF = jnp.bfloat16
MESH = pl.DeviceIdType.MESH
VMEM_LIMIT = 56 * 1024 * 1024

ALL = [(z, y, c) for z in range(4) for y in range(2) for c in range(2)]


def tp_of(z, y, c):
    return z * 4 + y * 2 + c


CORE_PAIRS = [(tp_of(z, y, c), tp_of(z, y, 1 - c)) for z, y, c in ALL]
Y_PAIRS = [(tp_of(z, y, c), tp_of(z, 1 - y, c)) for z, y, c in ALL]
Z_PAIRS = {k: [(tp_of(z, y, c), tp_of((z + k) % 4, y, c)) for z, y, c in ALL] for k in (1, 2, 3)}


def place():
    me = lax.axis_index('tp')
    return lax.div(me, 4), lax.rem(lax.div(me, 2), 2), lax.rem(me, 2)


def remote(src, dst, send_sem, recv_sem, dev):
    return pltpu.make_async_remote_copy(src_ref=src, dst_ref=dst, send_sem=send_sem, recv_sem=recv_sem,
                                        device_id={'tp': dev}, device_id_type=MESH)


def direct_exchange(both, x_ref, o_ref, send, recv):
    z, y, c = place()
    d = lax.axis_index('dp')
    peers = [(g, r, k) for g in range(1 + both) for r in range(4) for k in range(4)][1:]
    slot = (d if both else 0, 2 * c + y, z)

    def peer(g, r, k):
        pg, pz, py, pc = lax.rem(d + g, 2), lax.rem(z + k, 4), lax.rem(y + r % 2, 2), lax.rem(c + r // 2, 2)
        return {'dp': pg, 'tp': tp_of(pz, py, pc)}, (pg if both else 0, 2 * pc + py, pz)

    def copy(n, p, at, dev):
        return pltpu.make_async_remote_copy(src_ref=x_ref, dst_ref=o_ref.at[at], send_sem=send.at[n], recv_sem=recv.at[p],
                                            device_id=dev, device_id_type=MESH)

    def greets():
        barrier = pltpu.get_barrier_semaphore()
        for p in peers:
            pl.semaphore_signal(barrier, inc=1, device_id=peer(*p)[0], device_id_type=MESH)
        pl.semaphore_wait(barrier, len(peers))

    def start():
        for n, p in enumerate(peers):
            copy(n, p, slot, peer(*p)[0]).start()
        o_ref[slot] = x_ref[...]

    def end():
        for n, p in enumerate(peers):
            dev, at = peer(p[0], p[1], 4 - p[2])
            copy(n, p, at, dev).wait_recv()
        for n, p in enumerate(peers):
            copy(n, p, slot, peer(*p)[0]).wait_send()

    return greets, start, end


def small_gather_body(x_ref, o_ref, send, recv):
    for part in direct_exchange(0, x_ref, o_ref, send, recv):
        part()


def small_gather(x, cid):
    return pl.pallas_call(
        small_gather_body, out_shape=jax.ShapeDtypeStruct((1, 4, 4) + x.shape, x.dtype),
        in_specs=[pl.BlockSpec(memory_space=pltpu.VMEM)], out_specs=pl.BlockSpec(memory_space=pltpu.VMEM),
        scratch_shapes=[pltpu.SemaphoreType.DMA((15,)), pltpu.SemaphoreType.DMA((1, 4, 4))],
        compiler_params=pltpu.CompilerParams(collective_id=cid, has_side_effects=True))(x)[0]


def row_gather_body(both, x_ref, i_ref, o_ref, a_ref, up_s, dn_s, y_s, c_s, recv, isend, irecv):
    greets, ints_start, ints_end = direct_exchange(both, i_ref, a_ref, isend, irecv)
    z, y, c = place()
    me = tp_of(z, y, c)
    y_dev, c_dev = tp_of(z, 1 - y, c), tp_of(z, y, 1 - c)
    has_up, has_dn = z < 3, z > 0

    greets()
    q, qy = 2 * c + y, 2 * c + 1 - y
    quarter = [q, qy, 2 * (1 - c) + y, 2 * (1 - c) + 1 - y]

    def up(src, b):
        return remote(src, o_ref.at[q, b], up_s.at[b], recv.at[0, b], me + 4)

    def dn(src, b):
        return remote(src, o_ref.at[q, b], dn_s.at[b], recv.at[0, b], me - 4)

    def ycopy(src, b):
        return remote(src, o_ref.at[q, b], y_s.at[b], recv.at[1, b], y_dev)

    def ccopy(src, r, b):
        return remote(src, o_ref.at[quarter[r], b], c_s.at[r, b], recv.at[r + 2, b], c_dev)

    def landed(r, b):
        remote(x_ref, o_ref.at[quarter[r], b], c_s.at[0, b], recv.at[r, b], c_dev).wait_recv()

    pl.when(has_up)(lambda: up(x_ref, z).start())
    pl.when(has_dn)(lambda: dn(x_ref, z).start())
    ycopy(x_ref, z).start()
    ccopy(x_ref, 0, z).start()
    ints_start()
    o_ref[q, z] = x_ref[...]
    for k in (1, 2, 3):
        lo, hi = z - k, z + k

        @pl.when(lo >= 0)
        def _():
            landed(0, lo)
            pl.when(has_up)(lambda: up(o_ref.at[q, lo], lo).start())
            ycopy(o_ref.at[q, lo], lo).start()
            ccopy(o_ref.at[q, lo], 0, lo).start()

        @pl.when(hi <= 3)
        def _():
            landed(0, hi)
            pl.when(has_dn)(lambda: dn(o_ref.at[q, hi], hi).start())
            ycopy(o_ref.at[q, hi], hi).start()
            ccopy(o_ref.at[q, hi], 0, hi).start()
    for k in range(4):
        for b, ok in ((z - k, z - k >= 0), (z + k, z + k <= 3)) if k else ((z, z >= 0),):
            @pl.when(ok)
            def _():
                landed(1, b)
                ccopy(o_ref.at[qy, b], 1, b).start()
    for b in range(4):
        landed(2, b)
        landed(3, b)
    for b in range(4):
        pl.when(has_up & (z >= b))(lambda: up(o_ref.at[q, b], b).wait_send())
        pl.when(has_dn & (z <= b))(lambda: dn(o_ref.at[q, b], b).wait_send())
        ycopy(o_ref.at[q, b], b).wait_send()
        ccopy(o_ref.at[q, b], 0, b).wait_send()
        ccopy(o_ref.at[qy, b], 1, b).wait_send()
    ints_end()


def row_gather(x, cid, ints, both):
    vm = pl.BlockSpec(memory_space=pltpu.VMEM)
    dma = pltpu.SemaphoreType.DMA
    more = [ints]
    outs = [jax.ShapeDtypeStruct((4, 4) + x.shape, x.dtype)] + [jax.ShapeDtypeStruct((1 + both, 4, 4) + i.shape, i.dtype) for i in more]
    out = pl.pallas_call(
        functools.partial(row_gather_body, both), out_shape=outs,
        in_specs=[vm] * len(outs), out_specs=[vm] * len(outs),
        scratch_shapes=[dma((4,))] * 3 + [dma((2, 4)), dma((4, 4))] + [dma((16 * both + 15,)), dma((1 + both, 4, 4))],
        compiler_params=pltpu.CompilerParams(collective_id=cid, has_side_effects=True, vmem_limit_bytes=16 * 1024 * 1024),
        cost_estimate=cost(30_000_000_000, 32 * x.size))(x, *more)
    return out


NT = (((1,), (1,)), ((), ()))
TN = (((0,), (0,)), ((), ()))


def fixed(shape, **kw):
    at = tuple(0 for _ in shape)
    return pl.BlockSpec(shape, lambda *_: at, **kw)


def once(shape):
    return fixed(shape, pipeline_mode=pl.Buffered(1))


def cost(flops, data):
    return pl.CostEstimate(flops=flops, bytes_accessed=data, transcendentals=0)


def row_mean(v):
    return jnp.mean(v, axis=1, keepdims=True)


def columns(values, width=128):
    lane = lax.broadcasted_iota(jnp.int32, (values[0].shape[0], width), 1)
    out = jnp.zeros(lane.shape, F32)
    for n, v in enumerate(values):
        out = jnp.where(lane == n, v, out)
    return out


def logits_body(chunk, h_ref, e_ref, t_ref, g_ref, z_ref, s_ref, x_ref, scr):
    tm = h_ref.shape[0]
    vocab = e_ref.shape[0]
    tgt = t_ref[0].T[:tm, 0:1].astype(jnp.int32)
    lane = lax.broadcasted_iota(jnp.int32, (tm, 128), 1)
    cen = h_ref[...].astype(F32)
    mean = row_mean(cen)
    cen = cen - mean
    inv = lax.rsqrt(row_mean(cen * cen) + LN_EPS)
    x = (cen * inv * g_ref[0:1, :] + g_ref[1:2, :]).astype(BF)
    x_ref[...] = x
    m = s = t = None
    for j in range(vocab // chunk):
        z = lax.dot_general(x, e_ref[pl.ds(j * chunk, chunk), :], NT, preferred_element_type=F32)
        z_ref[:, pl.ds(j * chunk, chunk)] = z
        parts = [z[:, k * 128:(k + 1) * 128] for k in range(chunk // 128)]
        hits = [jnp.where(lane == tgt - (j * chunk + k * 128), p, 0.0) for k, p in enumerate(parts)]
        n = functools.reduce(jnp.maximum, parts if m is None else [m] + parts)
        add = functools.reduce(jnp.add, [jnp.exp(p - n) for p in parts])
        s = add if m is None else s * jnp.exp(m - n) + add
        t = functools.reduce(jnp.add, hits if t is None else [t] + hits)
        m = n
    mx = jnp.max(m, axis=1, keepdims=True)
    sm = jnp.sum(s * jnp.exp(m - mx), axis=1, keepdims=True)
    tt = jnp.sum(t, axis=1, keepdims=True)
    scr[...] = jnp.zeros_like(scr)
    scr[:tm, :] = columns((mx, sm, tt, mean, inv))
    s_ref[0] = scr[...].T[:8, :]


def logits_call(h, e, rows8, gain):
    b, d = h.shape
    v = e.shape[0]
    tm = b // 4
    row = pl.BlockSpec((tm, d), lambda i: (i, 0))
    stat = pl.BlockSpec((1, 8, 512), lambda i: (i, 0, 0))
    return pl.pallas_call(
        functools.partial(logits_body, 512), grid=(4,),
        in_specs=[row, once((v, d)), stat, fixed(gain.shape)],
        out_specs=[pl.BlockSpec((tm, v), lambda i: (i, 0)), stat, row],
        out_shape=[jax.ShapeDtypeStruct((b, v), F32), jax.ShapeDtypeStruct((4, 8, 512), F32), jax.ShapeDtypeStruct((b, d), BF)],
        scratch_shapes=[pltpu.VMEM((512, 128), F32)],
        compiler_params=pltpu.CompilerParams(vmem_limit_bytes=VMEM_LIMIT),
        cost_estimate=cost(2 * b * d * v, 4 * b * v))(h, e, rows8, gain)


def put_rows(val, c_ref, y_ref, o_ref):
    i = pl.program_id(0)
    for ok, ref in ((i < 2, c_ref), (i == 2, y_ref), (i == 3, o_ref)):
        @pl.when(ok)
        def _():
            ref[...] = val[...]


def norm_sums(acc, h_ref, cols, s_ref):
    tm = acc.shape[0]
    hat = (h_ref[...].astype(F32) - cols[:tm, 3:4]) * cols[:tm, 4:5]
    ds = jnp.sum(acc[...] * hat, axis=0, keepdims=True)
    dt = jnp.sum(acc[...], axis=0, keepdims=True)
    row = lax.broadcasted_iota(jnp.int32, s_ref.shape, 0)
    new = jnp.where(row == 0, ds, jnp.where(row == 1, dt, 0.0))

    @pl.when(pl.program_id(0) == 0)
    def _():
        s_ref[...] = new

    @pl.when(pl.program_id(0) > 0)
    def _():
        s_ref[...] += new


def grad_body(perm, z_ref, e_ref, r_ref, h_ref, dz_ref, c_ref, y_ref, o_ref, s_ref, acc):
    tm, v = z_ref.shape
    cols = r_ref[0].T
    lse, w, tgt = [cols[:tm, k:k + 1] for k in range(3)]
    tgt = tgt.astype(jnp.int32)
    lane = lax.broadcasted_iota(jnp.int32, (tm, 512), 1)
    for j in range(v // 512):
        p = jnp.exp(z_ref[:, j * 512:(j + 1) * 512] - lse)
        p = jnp.where(lane == tgt - j * 512, p - 1.0, p)
        dz_ref[:, j * 512:(j + 1) * 512] = (p * w).astype(BF)
    acc[...] = jnp.dot(dz_ref[...], e_ref[...], preferred_element_type=F32)
    put_rows(acc, c_ref, y_ref, o_ref)
    norm_sums(acc, h_ref, cols, s_ref)


def half_body(perm, z_ref, e_ref, r_ref, h_ref, c_ref, y_ref, o_ref, s_ref, acc):
    acc[...] = jnp.dot(z_ref[...], e_ref[...], preferred_element_type=F32)
    put_rows(acc, c_ref, y_ref, o_ref)
    norm_sums(acc, h_ref, r_ref[0].T, s_ref)


def grad_call(first, z, e, rows8, hid, perm):
    b, v = z.shape
    d = e.shape[1] // 2
    tm = b // 4
    half = 0 if first else 1
    row = pl.BlockSpec((tm, v), lambda i, p: (p[i], 0))
    outs = [pl.BlockSpec((tm, d), lambda i, p: (jnp.minimum(i, 1), 0)), fixed((tm, d)), fixed((tm, d)),
            fixed((8, d))]
    shapes = [jax.ShapeDtypeStruct((b // 2, d), F32), jax.ShapeDtypeStruct((b // 4, d), F32),
              jax.ShapeDtypeStruct((b // 4, d), F32), jax.ShapeDtypeStruct((8, d), F32)]
    return pl.pallas_call(
        grad_body if first else half_body,
        grid_spec=pltpu.PrefetchScalarGridSpec(
            num_scalar_prefetch=1, grid=(4,),
            in_specs=[row, pl.BlockSpec((v, d), lambda i, p: (0, half), pipeline_mode=pl.Buffered(1)),
                      pl.BlockSpec((1, 8, 512), lambda i, p: (p[i], 0, 0)),
                      pl.BlockSpec((tm, d), lambda i, p: (p[i], half))],
            out_specs=[row] * first + outs, scratch_shapes=[pltpu.VMEM((tm, d), F32)]),
        out_shape=[jax.ShapeDtypeStruct((b, v), BF)] * first + shapes,
        compiler_params=pltpu.CompilerParams(vmem_limit_bytes=VMEM_LIMIT),
        cost_estimate=cost(2 * b * d * v, 2 * b * v))(perm, z, e, rows8, hid)


def embed_body(a_ref, b_ref, xa_ref, xb_ref, o_ref):
    o_ref[...] = lax.dot_general(a_ref[...], xa_ref[...], TN, preferred_element_type=F32)
    o_ref[...] += lax.dot_general(b_ref[...], xb_ref[...], TN, preferred_element_type=F32)


def embed_call(da, db, xa, xb, half, into=None):
    v = da.shape[1]
    d = xa.shape[1]
    tv = 256
    n = v // tv // 2

    def body(*refs):
        embed_body(*refs[:4], refs[-1])

    def col(x):
        return pl.BlockSpec((x.shape[0], tv), lambda j: (0, half * n + j))

    def full(x):
        return once(x.shape)

    more = [] if into is None else [into]
    return pl.pallas_call(
        body, grid=(n,), in_specs=[col(da), col(db), full(xa), full(xb)] + [pl.BlockSpec(memory_space=pl.ANY) for _ in more],
        out_specs=pl.BlockSpec((tv, d), lambda j: (half * n + j, 0)), out_shape=jax.ShapeDtypeStruct((v, d), F32),
        input_output_aliases={4: 0} if more else {},
        compiler_params=pltpu.CompilerParams(vmem_limit_bytes=VMEM_LIMIT),
        cost_estimate=cost((da.shape[0] + db.shape[0]) * d * v, 4 * da.shape[0] * v))(da, db, xa, xb, *more)


def weight_body(h_ref, g_ref, o_ref):
    o_ref[...] = lax.dot_general(h_ref[...], g_ref[...], TN, preferred_element_type=F32)


def weight_call(h, g):
    t, d = h.shape
    tv = 256
    return pl.pallas_call(
        weight_body, grid=(d // tv,),
        in_specs=[pl.BlockSpec((t, tv), lambda j: (0, j)),
                  once((t, d))],
        out_specs=pl.BlockSpec((tv, d), lambda j: (j, 0)), out_shape=jax.ShapeDtypeStruct((d, d), F32),
        compiler_params=pltpu.CompilerParams(vmem_limit_bytes=VMEM_LIMIT),
        cost_estimate=cost(2 * t * d * d, 4 * d * d))(h, g)


def share_body(at, own, core, other, *rest):
    outs, scr = rest[:-1], rest[-1]
    scr[...] = own[...] + core[...] + other[...]
    for k, out in enumerate(outs):
        out[...] = scr[pl.ds(pl.multiple_of(at[k], 8), out.shape[0]), :]


def share_call(at, own, from_core, from_y, wide):
    n, d = own.shape
    return pl.pallas_call(
        share_body,
        grid_spec=pltpu.PrefetchScalarGridSpec(
            num_scalar_prefetch=1, grid=(1,),
            in_specs=[fixed((n, d)), pl.BlockSpec((n, d), lambda i, p: (1, 0)), fixed((n, d))],
            out_specs=[fixed((wide, d))] * 4, scratch_shapes=[pltpu.VMEM((n, d), F32)]),
        out_shape=[jax.ShapeDtypeStruct((wide, d), F32)] * 4,
        compiler_params=pltpu.CompilerParams(vmem_limit_bytes=VMEM_LIMIT),
        cost_estimate=cost(n * d * 2000, n * d * 20))(at, own, from_core, from_y)


def norm_back_body(*refs):
    l4, r4, pick, (a_ref, g_ref, da_ref, db_ref) = refs[:4], refs[4:8], refs[8:-4], refs[-4:]
    halves = [(p[0][...] + p[1][...]) + (p[2][...] + p[3][...]) for p in (l4, r4)]
    dy = jnp.concatenate(halves, axis=1)
    for sel in pick:
        dy = jnp.dot(sel[...], dy, precision=lax.Precision.HIGHEST, preferred_element_type=F32)
    a = a_ref[...].astype(F32)
    cen = a - row_mean(a)
    inv = lax.rsqrt(row_mean(cen * cen) + LN_EPS)
    hat = cen * inv
    dh = dy * g_ref[...]
    da = inv * (dh - row_mean(dh) - hat * row_mean(dh * hat))
    da_ref[...] = da
    db_ref[...] = da.astype(BF)


def norm_back(parts, pick, a, gain):
    t, d = a.shape
    vm = pl.BlockSpec(memory_space=pltpu.VMEM)
    return pl.pallas_call(
        norm_back_body, in_specs=[vm] * (10 + len(pick)), out_specs=[vm] * 2,
        out_shape=[jax.ShapeDtypeStruct((t, d), F32), jax.ShapeDtypeStruct((t, d), BF)],
        compiler_params=pltpu.CompilerParams(vmem_limit_bytes=24 * 1024 * 1024),
        cost_estimate=cost(1_000_000_000, 22 * t * d))(*parts, *pick, a, gain)


SIZES = ((1280, 384, 128), (1536, 448, 128), (2048, 512, 136))


def solution(mesh):
    tok_spec = P(('dp', 'tp'), None)
    row_spec = P(None, ('dp', 'tp'))

    def device_step(hidden, w_two, ln_scale, ln_shift, embed, targets, loss_mask):
        h_all, ints = row_gather(hidden, 1, jnp.concatenate([targets, loss_mask, jnp.zeros((4, targets.shape[1]), jnp.int32)], axis=0), 1)
        shares = jnp.sum(ints[:, :, :, 2:4], axis=-1)
        share_max = jnp.max(shares[..., 0])
        quarter_max = jnp.max(jnp.sum(shares[..., 0], axis=2))
        all_max = jnp.max(jnp.sum(shares[..., 1], axis=(1, 2)))
        fits = [(all_max <= rows) & (quarter_max <= cap) & (share_max + 7 <= wide) for rows, cap, wide in SIZES[:-1]]
        which = jnp.where(fits[0], 0, jnp.where(fits[1], 1, 2))
        args = (hidden, w_two, ln_scale, ln_shift, embed, h_all, ints[lax.axis_index('dp')])
        return lax.switch(which, [functools.partial(branch, n) for n in range(len(SIZES))], *args)

    def branch(n, *args):
        return step(n, *SIZES[n], *args)

    def step(num, cap_b, cap_a, wide_a, hidden, w_two, ln_scale, ln_shift, embed, h_all, ints):
        toks, width = hidden.shape
        span = 4 * toks
        cid = 10 * (num + 1)
        base = (lax.axis_index('tp') * embed.shape[0]).astype(F32)
        zi, yi, ci = place()
        mine = 2 * ci + yi
        ring = lax.rem(zi + jnp.arange(4, dtype=jnp.int32), 4)
        perm = jnp.stack([3 - mine, 2 * (1 - ci) + yi, 2 * ci + 1 - yi, mine])
        h_rows = h_all.reshape(4 * span, width)
        tri = (lax.broadcasted_iota(jnp.int32, (span, span), 0) < lax.broadcasted_iota(jnp.int32, (span, span), 1)).astype(BF)
        caps = (cap_a, cap_b // 4)

        def compact(h):
            cap = caps[h]
            mask = ints[:, :, 2 + h].reshape(4, span)
            rank = jnp.dot(mask.astype(BF), tri, preferred_element_type=F32).astype(jnp.int32)
            starts = rank[:, ::toks]
            count = jnp.sum(mask, axis=1)
            if h == 1:
                rank = rank + (jnp.cumsum(count) - count)[:, None]
            slot = jnp.where(mask > 0, rank, -1)
            row = lax.broadcasted_iota(jnp.int32, (4, cap, 1), 1)
            if h == 1:
                row = row + lax.broadcasted_iota(jnp.int32, (4, cap, 1), 0) * cap
                pick = (row.reshape(4 * cap, 1) == slot.reshape(1, -1)).astype(BF)
                contract = lambda rhs: jnp.dot(pick, rhs.reshape(4 * span, -1), preferred_element_type=F32).reshape(4, cap, -1)
            else:
                pick = (row == slot[:, None, :]).astype(BF)
                contract = lambda rhs: jnp.einsum('qrt,qtd->qrd', pick, rhs.reshape(4, span, -1), preferred_element_type=F32)
            tgt = ints[:, :, h].reshape(4, span)
            vals = jnp.stack([mask, lax.div(tgt, 256), lax.rem(tgt, 256)], axis=-1).astype(BF)
            got = jnp.swapaxes(contract(vals), 1, 2)
            got = jnp.pad(got, ((0, 0), (0, 0), (0, 512 - cap)))
            wgt = got[:, 0] / jnp.sum(count).astype(F32)
            tgt_row = got[:, 1] * 256.0 + got[:, 2] - base
            rows = contract(h_rows).astype(BF).reshape(4 * cap, width)
            return slot, starts, rows, wgt, tgt_row

        def pad8(*rows):
            return jnp.stack(list(rows) + [jnp.zeros_like(rows[0])] * (8 - len(rows)), axis=1)

        def statistics(h, rows, tgt_row, wgt):
            z, st, x = logits_call(rows, embed, pad8(tgt_row), jnp.stack([ln_scale[h], ln_shift[h]]))
            s = jnp.where(st[:, 1] > 0.0, st[:, 1], 1.0)
            part = jnp.concatenate([(st[:, 0] + jnp.log(s)).reshape(16, 128), st[:, 2].reshape(16, 128)], axis=0)
            parts = small_gather(part, cid + h).reshape(16, 2, 4, 512)
            top = jnp.max(parts[:, 0], axis=0)
            lse = top + jnp.log(jnp.sum(jnp.exp(parts[:, 0] - top), axis=0))
            return x, z, pad8(lse, wgt, tgt_row, st[:, 3], st[:, 4]), lse - jnp.sum(parts[:, 1], axis=0)

        def own_slots(slot):
            return lax.dynamic_slice_in_dim(slot[mine], zi * toks, toks)

        def own_rows(h, slot):
            own = own_slots(slot)
            return jnp.where(own >= 0, own + (mine * caps[0] if h == 0 else 0), -1)

        def losses(h, slot, raw, wgt):
            flat = raw[:, :caps[h]].reshape(1, -1)
            hit = own_rows(h, slot)[:, None] == lax.broadcasted_iota(jnp.int32, (toks, flat.shape[1]), 1)
            return jnp.sum(jnp.where(hit, flat, 0.0), axis=1), jnp.sum(raw * wgt)

        def exchange(begins, wide, to_core, to_y, own):
            n = own.shape[0]
            from_core = lax.ppermute(to_core, 'tp', CORE_PAIRS)
            send = to_y + from_core[:n]
            from_y = lax.ppermute(send, 'tp', Y_PAIRS)
            parts = list(share_call(begins, own, from_core, from_y, wide))
            for k in Z_PAIRS:
                parts[k] = lax.ppermute(parts[k], 'tp', Z_PAIRS[k])
            return parts

        def halves(z, rows8, hid, begins, wide):
            dz, *left, sum_l = grad_call(1, z, embed, rows8, hid, perm)
            *right, sum_r = grad_call(0, dz, embed, rows8, hid, perm)
            return dz, exchange(begins, wide, *left) + exchange(begins, wide, *right), right[2], jnp.concatenate([sum_l, sum_r], axis=1)

        slot_b, _, hid_b, wgt_b, tgt_b = compact(1)
        proj_b = jnp.dot(hid_b, w_two, preferred_element_type=F32).astype(BF)
        x_b, z_b, rows_b, raw_b = statistics(1, proj_b, tgt_b, wgt_b)
        loss_b, tot_b = losses(1, slot_b, raw_b, wgt_b)
        wide_b = cap_b // 16
        dz_b, parts_b, last_b, sums_b = halves(z_b, rows_b, proj_b, ring * wide_b, wide_b)

        slot_a, starts_a, hid_a, wgt_a, tgt_a = compact(0)
        hid_a, slot_a, starts_a, _ = lax.optimization_barrier((hid_a, slot_a, starts_a, last_b))
        starts_a = jnp.minimum(starts_a - lax.rem(starts_a, 8), cap_a - wide_a)[mine]
        begins_a = jnp.take(starts_a, ring)
        at = own_slots(slot_a)
        at = jnp.where(at >= 0, at - begins_a[0], -1)
        pick_a = (at[:, None] == lax.broadcasted_iota(jnp.int32, (toks, wide_a), 1)).astype(F32)
        hid_a, begins_a, pick_a = lax.optimization_barrier((hid_a, begins_a, pick_a))
        x_a, z_a, rows_a, raw_a = statistics(0, hid_a, tgt_a, wgt_a)
        loss_a, tot_a = losses(0, slot_a, raw_a, wgt_a)
        dz_a, parts_a, _, sums_a = halves(z_a, rows_a, hid_a, begins_a, wide_a)
        d_embed = embed_call(dz_a, dz_b, x_a, x_b, 0)
        d_embed = embed_call(dz_a, dz_b, x_a, x_b, 1, d_embed)

        own_b = lax.dynamic_slice_in_dim(proj_b, mine * caps[1] + zi * wide_b, wide_b)
        _, d_proj = norm_back(parts_b, [], own_b, ln_scale[1:2])
        ln_part = jnp.concatenate([v.reshape(-1, 128) for v in (sums_a[0], sums_b[0], sums_a[1], sums_b[1])], axis=0)
        g_all, ln_all = row_gather(d_proj, cid + 2, ln_part, 0)
        g_all = g_all.reshape(cap_b, width)
        ln_all = jnp.sum(ln_all.reshape(16, 4, width), axis=0)
        d_w_two = weight_call(hid_b, g_all)
        pick_b = (own_rows(1, slot_b)[:, None] == lax.broadcasted_iota(jnp.int32, (toks, cap_b), 1)).astype(BF)
        d_own = jnp.dot(pick_b, g_all, preferred_element_type=F32).astype(BF)
        via_two = lax.dot_general(d_own, w_two, NT, preferred_element_type=F32)
        da_a, _ = norm_back(parts_a, [pick_a], hidden, ln_scale[0:1])
        d_hidden = (da_a + via_two).astype(BF)
        token_loss = jnp.stack([loss_a, loss_b])
        return token_loss, (tot_a + tot_b).reshape(1), d_hidden, d_embed, d_w_two, ln_all[:2], ln_all[2:]

    return jax.shard_map(device_step, mesh=mesh,
                         in_specs=(tok_spec, P(), P(), P(), P('tp', None), row_spec, row_spec),
                         out_specs=(row_spec, P('dp'), tok_spec, tok_spec, P('dp', None), P('dp', None), P('dp', None)),
                         check_vma=False)
```

time: 1080 us -> 660 us (0.61)
  the two profiles are of different devices: /device:TPU:0 before, /device:TPU:8 now
where the time goes in v2:
time: 660 us; the launch traced here: 650 us
  Pallas kernels  399 us (60%)
  waiting for transfers between devices  125 us (19%)
  matrix products  47.8 us (7%)
  starting transfers between devices  22.6 us (3%)
  other arithmetic  21.8 us (3%)
  local copies, waits for them, and re-layouts  16.6 us (3%)
  loops' own time  11.7 us (2%)
    pallas_call x2, Pallas kernels, row_gather(): pl.pallas_call(functools.partial(row_gather_body, both), out_shape=outs,...  138 us
    pallas_call x4, Pallas kernels, grad_call(): pl.pallas_call(grad_body if first else half_body, grid_spec=pltpu.Prefetc...  85.3 us
    ppermute x12, waiting for transfers between devices, exchange(): parts[k] = lax.ppermute(parts[k], 'tp', Z_PAIRS[k])  83.9 us
    pallas_call x2, Pallas kernels, logits_call(): pl.pallas_call(functools.partial(logits_body, 512), grid=(4,), in_specs=[...  61.4 us
    pallas_call x2, Pallas kernels, embed_call(): pl.pallas_call(body, grid=(n,), in_specs=[col(da), col(db), full(xa), ful...  50.5 us
    ppermute x4, waiting for transfers between devices, exchange(): from_y = lax.ppermute(send, 'tp', Y_PAIRS)  41.3 us
    pallas_call x2, Pallas kernels, small_gather(): pl.pallas_call(small_gather_body, out_shape=jax.ShapeDtypeStruct((1, 4, 4...  24.9 us
    pallas_call x4, Pallas kernels, share_call(): pl.pallas_call(share_body, grid_spec=pltpu.PrefetchScalarGridSpec(num_sca...  17.6 us
  transfers between devices with their start and end apart: 20, of which 11 were waited for; matrix products, arithmetic and copies ran while one was open for 6% of the time, Pallas kernels for 42%

profile of v2, /device:TPU:8, one launch (start us, length us, event | category | flops | bytes accessed | tf_op | source)
XLA Modules:
  0.0 650.0 jit_solution(17392121601519463944)
XLA Ops:
  1.5 60.2 %shard_map.126 = (bf16[4,4,128,2048]{3,2,1,0:T(8,128)(2,1)}, s32[2,4,4,8,128]{4,3,2,1,0:T(8,128)S(1)}) custom-call(bf16[128,2048]{1,0:T(8,128)(2,1)} %x_ref.1, s32[8,128]{1,0:T(8,128)S(1)} %add_add_fusion.i_ref), custom_call_target="tpu_custom_call" | custom-call | flops 30000001024 | bytes 8388608 | tf_op jit(solution)/shard_map/pallas_call | solution.py:156
  67.7 580.2 %conditional.4 = (f32[2,128]{1,0:T(2,128)}, f32[1]{0:T(128)}, f32[3072,2048]{1,0:T(8,128)}, f32[2048,2048]{1,0:T(8,128)}, f32[2,2048]{1,0:T(2,128)}, /*index=5*/f32[2,2048]{1,0:T(2,128)}, bf16[128,2048]{1,0:T(8,128)(2,1)S(1)}) conditional(s32[]{:T(128)} %clamp.27, (s32[]{:T(128)}, s32[2,4,4,8,128]{4,3,2,1,0:T(8,128)S(1)}, ...), branch_computations={%region_6.23_spmd, %region_22.39_spmd, %region_38.55_spmd} | conditional | flops 248859869184 | bytes 639518656
  71.9 13.7 %fusion.8 = bf16[4,320,2048]{2,1,0:T(8,128)(2,1)S(1)} fusion(bf16[2048,2048,1]{1,0,2:T(8,128)(2,1)} %bitcast.421, s32[2048]{0:T(1024)S(1)} %bitcast.403, s32[4,320]{1,0:T(4,128)S(1)} %iota_add_fusion), kind=kOutput, calls=%fused_computation.13 | convolution fusion | flops 10742661120 | bytes 13644800 | tf_op jit(solution)/shard_map/cond/branch_0_fun/dot_general | solution.py:447
  85.7 12.6 %convolution_convert_fusion.h_ref = bf16[1280,2048]{1,0:T(8,128)(2,1)} fusion(bf16[1280,2048]{1,0:T(8,128)(2,1)S(1)} %bitcast.434, bf16[2048,2048]{1,0:T(8,128)(2,1)S(1)} %copy-done.25), kind=kOutput, calls=%fused_computation.7 | convolution fusion | flops 10740039680 | bytes 18874368 | tf_op jit(solution)/shard_map/cond/branch_0_fun/dot_general | solution.py:500
  98.3 1.7 fusion.14
  101.5 28.5 %branch_0_fun.18 = (f32[1280,3072]{1,0:T(8,128)}, f32[4,8,512]{2,1,0:T(8,128)}, bf16[1280,2048]{1,0:T(8,128)(2,1)}) custom-call(bf16[1280,2048]{1,0:T(8,128)(2,1)} %convolution_convert_fusion.h_ref, bf16[3072,2048]{1,0:T(8,128)(2,1)} %get-tuple-element.101.e_ref, f32[4,8,512]{2,1,0:T(8,128)} %get-tuple-element.506.t_ref, f32[2,2048]{1,0:T(2,128)} %pad_maximum_fusion.5.g_ref), custom_call_target="tpu_custom_call" | custom-call | flops 16106127360 | bytes 15728640 | tf_op jit(solution)/shard_map/cond/branch_0_fun/pallas_call | solution.py:230
  132.5 13.2 %branch_0_fun.19 = f32[1,4,4,32,128]{4,3,2,1,0:T(8,128)} custom-call(f32[32,128]{1,0:T(8,128)} %pad_maximum_fusion.6.x_ref), custom_call_target="tpu_custom_call" | custom-call | tf_op jit(solution)/shard_map/cond/branch_0_fun/pallas_call | solution.py:78
  148.7 22.3 %branch_0_fun.20 = (bf16[1280,3072]{1,0:T(8,128)(2,1)}, f32[640,1024]{1,0:T(8,128)}, f32[320,1024]{1,0:T(8,128)}, f32[320,1024]{1,0:T(8,128)}, f32[8,1024]{1,0:T(8,128)}) custom-call(s32[4]{0:T(128)} %get-tuple-element.528.perm, f32[1280,3072]{1,0:T(8,128)} %get-tuple-element.104.z_ref, bf16[3072,2048]{1,0:T(8,128)(2,1)} %get-tuple-element.101.e_ref, ...), custom_call_target="tpu_custom_call" | custom-call | flops 8053063680 | bytes 7864320 | tf_op jit(solution)/shard_map/cond/branch_0_fun/pallas_call | solution.py:296
  171.6 17.5 %branch_0_fun.21 = (f32[640,1024]{1,0:T(8,128)}, f32[320,1024]{1,0:T(8,128)}, f32[320,1024]{1,0:T(8,128)}, f32[8,1024]{1,0:T(8,128)}) custom-call(s32[4]{0:T(128)} %get-tuple-element.528.perm, bf16[1280,3072]{1,0:T(8,128)(2,1)} %get-tuple-element.106.z_ref.refs_1_, bf16[3072,2048]{1,0:T(8,128)(2,1)} %get-tuple-element.101.e_ref, f32[4,8,512]{2,1,0:T(8,128)} %stack.119.r_ref, ...), custom_call_target="tpu_custom_call" | custom-call | flops 8053063680 | bytes 7864320 | tf_op jit(solution)/shard_map/cond/branch_0_fun/pallas_call | solution.py:296
  189.2 9.1 %convolution_convert_fusion.1 = bf16[4,384,2048]{2,1,0:T(8,128)(2,1)} fusion(bf16[4,512,2048]{2,1,0:T(8,128)(2,1)} %bitcast.422, s32[4,512]{1,0:T(4,128)S(1)} %get-tuple-element.108), kind=kOutput, calls=%fused_computation.12 | convolution fusion | flops 3225157632 | bytes 14688256 | tf_op jit(solution)/shard_map/cond/branch_0_fun/qrt,qtd->qrd/dot_general | solution.py:450
  199.8 33.0 %branch_0_fun.22 = (f32[1536,3072]{1,0:T(8,128)}, f32[4,8,512]{2,1,0:T(8,128)}, bf16[1536,2048]{1,0:T(8,128)(2,1)}) custom-call(bf16[1536,2048]{1,0:T(8,128)(2,1)} %bitcast.352, bf16[3072,2048]{1,0:T(8,128)(2,1)} %get-tuple-element.101.e_ref, f32[4,8,512]{2,1,0:T(8,128)} %get-tuple-element.505.t_ref, f32[2,2048]{1,0:T(2,128)} %pad_maximum_fusion.7.g_ref), custom_call_target="tpu_custom_call" | custom-call | flops 19327352832 | bytes 18874368 | tf_op jit(solution)/shard_map/cond/branch_0_fun/pallas_call | solution.py:230
  235.2 11.7 %branch_0_fun.23 = f32[1,4,4,32,128]{4,3,2,1,0:T(8,128)} custom-call(f32[32,128]{1,0:T(8,128)} %pad_maximum_fusion.8.x_ref), custom_call_target="tpu_custom_call" | custom-call | tf_op jit(solution)/shard_map/cond/branch_0_fun/pallas_call | solution.py:78
  249.4 25.7 %branch_0_fun.24 = (bf16[1536,3072]{1,0:T(8,128)(2,1)}, f32[768,1024]{1,0:T(8,128)}, f32[384,1024]{1,0:T(8,128)}, f32[384,1024]{1,0:T(8,128)}, f32[8,1024]{1,0:T(8,128)}) custom-call(s32[4]{0:T(128)} %get-tuple-element.528.perm, f32[1536,3072]{1,0:T(8,128)} %get-tuple-element.113.z_ref, bf16[3072,2048]{1,0:T(8,128)(2,1)} %get-tuple-element.101.e_ref, ...), custom_call_target="tpu_custom_call" | custom-call | flops 9663676416 | bytes 9437184 | tf_op jit(solution)/shard_map/cond/branch_0_fun/pallas_call | solution.py:296
  275.5 19.8 %branch_0_fun.30 = (f32[768,1024]{1,0:T(8,128)}, f32[384,1024]{1,0:T(8,128)}, f32[384,1024]{1,0:T(8,128)}, f32[8,1024]{1,0:T(8,128)}) custom-call(s32[4]{0:T(128)} %get-tuple-element.528.perm, bf16[1536,3072]{1,0:T(8,128)(2,1)} %get-tuple-element.114.refs_0_.z_ref, bf16[3072,2048]{1,0:T(8,128)(2,1)} %get-tuple-element.101.e_ref, f32[4,8,512]{2,1,0:T(8,128)} %stack.126.r_ref, ...), custom_call_target="tpu_custom_call" | custom-call | flops 9663676416 | bytes 9437184 | tf_op jit(solution)/shard_map/cond/branch_0_fun/pallas_call | solution.py:296
  295.5 25.2 %branch_0_fun.25.refs_4_ = f32[3072,2048]{1,0:T(8,128)} custom-call(bf16[1536,3072]{1,0:T(8,128)(2,1)} %get-tuple-element.114.refs_0_.z_ref, bf16[1280,3072]{1,0:T(8,128)(2,1)} %get-tuple-element.106.z_ref.refs_1_, bf16[1536,2048]{1,0:T(8,128)(2,1)} %get-tuple-element.115.refs_2_, bf16[1280,2048]{1,0:T(8,128)(2,1)} %get-tuple-element.116.refs_3_), custom_call_target="tpu_custom_call" | custom-call | flops 17716740096 | bytes 18874368 | tf_op jit(solution)/shard_map/cond/branch_0_fun/pallas_call | solution.py:330
  320.7 25.3 %branch_0_fun.26 = f32[3072,2048]{1,0:T(8,128)} custom-call(bf16[1536,3072]{1,0:T(8,128)(2,1)} %get-tuple-element.114.refs_0_.z_ref, bf16[1280,3072]{1,0:T(8,128)(2,1)} %get-tuple-element.106.z_ref.refs_1_, bf16[1536,2048]{1,0:T(8,128)(2,1)} %get-tuple-element.115.refs_2_, ...), custom_call_target="tpu_custom_call", output_to_operand_aliasing={{}: (4, {})} | custom-call | flops 17716740096 | bytes 18874368 | tf_op jit(solution)/shard_map/cond/branch_0_fun/pallas_call | solution.py:330
  348.8 1.9 slice_add_fusion.3
  350.8 1.4 collective-permute-start.1
  356.3 26.2 %collective-permute-done.1.other = f32[320,1024]{1,0:T(8,128)S(1)} collective-permute-done((f32[320,1024]{1,0:T(8,128)S(1)}, f32[320,1024]{1,0:T(8,128)S(1)}, u32[]{:S(2)}, u32[]{:S(2)}) %collective-permute-start.1) | collective-permute-done | bytes 1310752 | tf_op jit(solution)/shard_map/cond/branch_0_fun/ppermute | solution.py:488
  383.6 4.1 branch_0_fun.27
  388.8 3.0 slice_add_fusion.1
  391.8 2.4 collective-permute-start.3
  394.9 15.1 %collective-permute-done.6.other = f32[320,1024]{1,0:T(8,128)} collective-permute-done((f32[320,1024]{1,0:T(8,128)}, f32[320,1024]{1,0:T(8,128)}, u32[]{:S(2)}, u32[]{:S(2)}) %collective-permute-start.6) | collective-permute-done | bytes 1310752 | tf_op jit(solution)/shard_map/cond/branch_0_fun/ppermute | solution.py:488
  410.0 4.1 branch_0_fun.28
  415.4 2.4 collective-permute-start.8
  418.5 2.9 slice_add_fusion
  421.5 1.3 collective-permute-start.11
  422.8 10.2 %collective-permute-done.4.refs_3_ = f32[80,1024]{1,0:T(8,128)S(1)} collective-permute-done((f32[80,1024]{1,0:T(8,128)S(1)}, f32[80,1024]{1,0:T(8,128)S(1)}, u32[]{:S(2)}, u32[]{:S(2)}) %collective-permute-start.4) | collective-permute-done | bytes 327712 | tf_op jit(solution)/shard_map/cond/branch_0_fun/ppermute | solution.py:491
  433.0 1.3 collective-permute-start.16
  434.4 4.1 collective-permute-done.7.refs_5_
  438.5 6.1 collective-permute-done.8.refs_6_
  444.5 2.7 collective-permute-done.9.refs_7_
  447.3 1.4 branch_0_fun.29
  448.7 77.4 %branch_0_fun.31 = (bf16[4,4,80,2048]{3,2,1,0:T(8,128)(2,1)S(1)}, f32[1,4,4,64,128]{4,3,2,1,0:T(8,128)S(1)}) custom-call(bf16[80,2048]{1,0:T(8,128)(2,1)S(1)} %get-tuple-element.130.x_ref, f32[64,128]{1,0:T(8,128)S(1)} %pad_maximum_fusion.4.i_ref), custom_call_target="tpu_custom_call" | custom-call | flops 30000001024 | bytes 5242880 | tf_op jit(solution)/shard_map/cond/branch_0_fun/pallas_call | solution.py:156
  526.1 2.3 copy-done.2
  529.6 4.7 branch_0_fun.33
  535.6 16.8 %branch_0_fun.32 = f32[2048,2048]{1,0:T(8,128)} custom-call(bf16[1280,2048]{1,0:T(8,128)(2,1)} %bitcast.435, bf16[1280,2048]{1,0:T(8,128)(2,1)} %bitcast.347), custom_call_target="tpu_custom_call" | custom-call | flops 10737418240 | bytes 16777216 | tf_op jit(solution)/shard_map/cond/branch_0_fun/pallas_call | solution.py:345
  553.7 2.3 collective-permute-start.13
  556.0 4.7 branch_0_fun.34
  560.7 2.0 collective-permute-start.17
  562.7 2.4 collective-permute-start.18
  565.1 9.7 %fusion.19 = f32[128,2048]{1,0:T(8,128)} fusion(bf16[2048,2048]{1,0:T(8,128)(2,1)} %get-tuple-element.100, bf16[1280,2048]{1,0:T(8,128)(2,1)} %bitcast.348, s32[128]{0:T(128)S(1)} %compare_select_fusion.9), kind=kOutput, calls=%fused_computation.32 | convolution fusion | flops 1745256448 | bytes 14680576 | tf_op jit(solution)/shard_map/cond/branch_0_fun/dot_general | solution.py:529
  574.8 14.8 %collective-permute-done.13.refs_2_ = f32[128,1024]{1,0:T(8,128)S(1)} collective-permute-done((f32[128,1024]{1,0:T(8,128)}, f32[128,1024]{1,0:T(8,128)S(1)}, u32[]{:S(2)}, u32[]{:S(2)}) %collective-permute-start.13) | collective-permute-done | bytes 524320 | tf_op jit(solution)/shard_map/cond/branch_0_fun/ppermute | solution.py:491
  589.6 24.3 %collective-permute-done.14.refs_3_ = f32[128,1024]{1,0:T(8,128)S(1)} collective-permute-done((f32[128,1024]{1,0:T(8,128)}, f32[128,1024]{1,0:T(8,128)S(1)}, u32[]{:S(2)}, u32[]{:S(2)}) %collective-permute-start.14) | collective-permute-done | bytes 524320 | tf_op jit(solution)/shard_map/cond/branch_0_fun/ppermute | solution.py:491
  613.8 9.1 %collective-permute-done.17.refs_5_ = f32[128,1024]{1,0:T(8,128)S(1)} collective-permute-done((f32[128,1024]{1,0:T(8,128)}, f32[128,1024]{1,0:T(8,128)S(1)}, u32[]{:S(2)}, u32[]{:S(2)}) %collective-permute-start.17) | collective-permute-done | bytes 524320 | tf_op jit(solution)/shard_map/cond/branch_0_fun/ppermute | solution.py:491
  622.9 11.2 %collective-permute-done.18.refs_6_ = f32[128,1024]{1,0:T(8,128)} collective-permute-done((f32[128,1024]{1,0:T(8,128)}, f32[128,1024]{1,0:T(8,128)}, u32[]{:S(2)}, u32[]{:S(2)}) %collective-permute-start.18) | collective-permute-done | bytes 524320 | tf_op jit(solution)/shard_map/cond/branch_0_fun/ppermute | solution.py:491
  634.1 1.4 collective-permute-done.19.refs_7_
  635.5 3.6 branch_0_fun.35
  (158 shorter events, 36.2 us)
Async XLA Ops:
  1.5 66.2 %copy-start.50 = (f32[2,2048]{1,0:T(2,128)S(1)}, f32[2,2048]{1,0:T(2,128)}, u32[]{:S(2)}) copy-start(f32[2,2048]{1,0:T(2,128)} %param.14) | copy-start | bytes 49156
  1.5 66.2 %copy-start.51 = (f32[2,2048]{1,0:T(2,128)S(1)}, f32[2,2048]{1,0:T(2,128)}, u32[]{:S(2)}) copy-start(f32[2,2048]{1,0:T(2,128)} %param.15) | copy-start | bytes 49156
  70.3 15.4 %copy-start.67 = (s32[4,512]{1,0:T(4,128)}, s32[4,512]{1,0:T(4,128)S(1)}, u32[]{:S(2)}) copy-start(s32[4,512]{1,0:T(4,128)S(1)} %fusion.18) | copy-start | bytes 24580
  71.2 0.6 copy-start.17
  71.9 13.8 %copy-start.25 = (bf16[2048,2048]{1,0:T(8,128)(2,1)S(1)}, bf16[2048,2048]{1,0:T(8,128)(2,1)}, u32[]{:S(2)}) copy-start(bf16[2048,2048]{1,0:T(8,128)(2,1)} %get-tuple-element.100) | copy-start | bytes 25165828
  85.7 12.7 %copy-start.75 = (bf16[4,320,2048]{2,1,0:T(8,128)(2,1)}, bf16[4,320,2048]{2,1,0:T(8,128)(2,1)S(1)}, u32[]{:S(2)}) copy-start(bf16[4,320,2048]{2,1,0:T(8,128)(2,1)S(1)} %fusion.8) | copy-start | bytes 15728644
  171.0 177.8 %collective-permute-start = (f32[640,1024]{1,0:T(8,128)}, f32[640,1024]{1,0:T(8,128)}, u32[]{:S(2)}, u32[]{:S(2)}) collective-permute-start(f32[640,1024]{1,0:T(8,128)} %get-tuple-element.118), channel_id=1, source_target_pairs={{0,1},{1,0},{2,3},{3,2},{4,5},{5,4},{6,7},{7,6},{8,9},{9,8},{10,11... | collective-permute-start | bytes 7864328 | tf_op jit(solution)/shard_map/cond/branch_0_fun/ppermute | solution.py:486
  189.1 163.7 %collective-permute-start.5 = (f32[640,1024]{1,0:T(8,128)}, f32[640,1024]{1,0:T(8,128)S(1)}, u32[]{:S(2)}, u32[]{:S(2)}) collective-permute-start(f32[640,1024]{1,0:T(8,128)} %get-tuple-element.124), channel_id=1, source_target_pairs={{0,1},{1,0},{2,3},{3,2},{4,5},{5,4},{6,7},{7,6},{8,9},{9,8},{10,11... | collective-permute-start | bytes 7864328 | tf_op jit(solution)/shard_map/cond/branch_0_fun/ppermute | solution.py:486
  199.0 33.8 %copy-start.68 = (s32[4]{0:T(128)}, s32[4]{0:T(128)S(1)}, u32[]{:S(2)}) copy-start(s32[4]{0:T(128)S(1)} %and_select_fusion.at) | copy-start | bytes 52
  275.1 113.7 %collective-permute-start.10 = (f32[768,1024]{1,0:T(8,128)}, f32[768,1024]{1,0:T(8,128)}, u32[]{:S(2)}, u32[]{:S(2)}) collective-permute-start(f32[768,1024]{1,0:T(8,128)} %get-tuple-element.139), channel_id=1, source_target_pairs={{0,1},{1,0},{2,3},{3,2},{4,5},{5,4},{6,7},{7,6},{8,9},{9,8},{10,11... | collective-permute-start | bytes 9437192 | tf_op jit(solution)/shard_map/cond/branch_0_fun/ppermute | solution.py:486
  295.3 120.1 %collective-permute-start.15 = (f32[768,1024]{1,0:T(8,128)}, f32[768,1024]{1,0:T(8,128)}, u32[]{:S(2)}, u32[]{:S(2)}) collective-permute-start(f32[768,1024]{1,0:T(8,128)} %get-tuple-element.146), channel_id=1, source_target_pairs={{0,1},{1,0},{2,3},{3,2},{4,5},{5,4},{6,7},{7,6},{8,9},{9,8},{10,11... | collective-permute-start | bytes 9437192 | tf_op jit(solution)/shard_map/cond/branch_0_fun/ppermute | solution.py:486
  320.7 26.7 %copy-start.55 = (f32[8,1024]{1,0:T(8,128)S(1)}, f32[8,1024]{1,0:T(8,128)}, u32[]{:S(2)}) copy-start(f32[8,1024]{1,0:T(8,128)} %get-tuple-element.133) | copy-start | bytes 98308
  320.7 26.7 %copy-start.61 = (f32[8,1024]{1,0:T(8,128)S(1)}, f32[8,1024]{1,0:T(8,128)}, u32[]{:S(2)}) copy-start(f32[8,1024]{1,0:T(8,128)} %get-tuple-element.131) | copy-start | bytes 98308
  320.7 27.6 %copy-start.56 = (f32[8,1024]{1,0:T(8,128)S(1)}, f32[8,1024]{1,0:T(8,128)}, u32[]{:S(2)}) copy-start(f32[8,1024]{1,0:T(8,128)} %get-tuple-element.134) | copy-start | bytes 98308
  320.7 27.6 %copy-start.62 = (f32[8,1024]{1,0:T(8,128)S(1)}, f32[8,1024]{1,0:T(8,128)}, u32[]{:S(2)}) copy-start(f32[8,1024]{1,0:T(8,128)} %get-tuple-element.132) | copy-start | bytes 98308
  347.4 5.3 copy-start.47
  350.8 31.7 %collective-permute-start.1 = (f32[320,1024]{1,0:T(8,128)S(1)}, f32[320,1024]{1,0:T(8,128)S(1)}, u32[]{:S(2)}, u32[]{:S(2)}) collective-permute-start(f32[320,1024]{1,0:T(8,128)S(1)} %slice_add_fusion.3), channel_id=1, source_target_pairs={{0,2},{1,3},{2,0},{3,1},{4,6},{5,7},{6,4},{7,5},{8,10},{9,11},{10,... | collective-permute-start | bytes 3932168 | tf_op jit(solution)/shard_map/cond/branch_0_fun/ppermute | solution.py:488
  352.7 2.5 copy-start.29
  352.7 36.1 %copy-start.43 = (f32[384,1024]{1,0:T(8,128)S(1)}, f32[384,1024]{1,0:T(8,128)}, u32[]{:S(2)}) copy-start(f32[384,1024]{1,0:T(8,128)} %get-tuple-element.140) | copy-start | bytes 4718596
  354.0 56.0 %collective-permute-start.6 = (f32[320,1024]{1,0:T(8,128)}, f32[320,1024]{1,0:T(8,128)}, u32[]{:S(2)}, u32[]{:S(2)}) collective-permute-start(f32[320,1024]{1,0:T(8,128)} %slice_add_fusion.2), channel_id=1, source_target_pairs={{0,2},{1,3},{2,0},{3,1},{4,6},{5,7},{6,4},{7,5},{8,10},{9,11},{10,... | collective-permute-start | bytes 3932168 | tf_op jit(solution)/shard_map/cond/branch_0_fun/ppermute | solution.py:488
  382.5 1.1 copy-start.48
  387.6 4.2 copy-start.72
  387.6 6.5 %copy-start.71 = (f32[80,1024]{1,0:T(8,128)S(1)}, f32[80,1024]{1,0:T(8,128)}, u32[]{:S(2)}) copy-start(f32[80,1024]{1,0:T(8,128)} %get-tuple-element.123) | copy-start | bytes 983044
  387.6 30.1 %collective-permute-start.2 = (f32[80,1024]{1,0:T(8,128)}, f32[80,1024]{1,0:T(8,128)S(1)}, u32[]{:S(2)}, u32[]{:S(2)}) collective-permute-start(f32[80,1024]{1,0:T(8,128)} %get-tuple-element.121), channel_id=1, source_target_pairs={{0,4},{1,5},{2,6},{3,7},{4,8},{5,9},{6,10},{7,11},{8,12},{9,13},{1... | collective-permute-start | bytes 983048 | tf_op jit(solution)/shard_map/cond/branch_0_fun/ppermute | solution.py:491
  388.8 29.7 %copy-start.42 = (f32[384,1024]{1,0:T(8,128)S(1)}, f32[384,1024]{1,0:T(8,128)}, u32[]{:S(2)}) copy-start(f32[384,1024]{1,0:T(8,128)} %get-tuple-element.147) | copy-start | bytes 4718596
  391.8 29.6 %collective-permute-start.3 = (f32[80,1024]{1,0:T(8,128)S(1)}, f32[80,1024]{1,0:T(8,128)S(1)}, u32[]{:S(2)}, u32[]{:S(2)}) collective-permute-start(f32[80,1024]{1,0:T(8,128)S(1)} %copy-done.72), channel_id=1, source_target_pairs={{0,8},{1,9},{2,10},{3,11},{4,12},{5,13},{6,14},{7,15},{8,0},{9,1},... | collective-permute-start | bytes 983048 | tf_op jit(solution)/shard_map/cond/branch_0_fun/ppermute | solution.py:491
  394.2 53.1 %copy-start.18 = (f32[1,2048]{1,0:T(1,128)S(1)}, f32[1,2048]{1,0:T(1,128)}, u32[]{:S(2)}) copy-start(f32[1,2048]{1,0:T(1,128)} %copy-done.17) | copy-start | bytes 24580
  394.2 53.1 %copy-start.23 = (f32[80,1024]{1,0:T(8,128)S(1)}, f32[80,1024]{1,0:T(8,128)}, u32[]{:S(2)}) copy-start(f32[80,1024]{1,0:T(8,128)} %get-tuple-element.120.refs_0_) | copy-start | bytes 983044
  394.2 38.8 %collective-permute-start.4 = (f32[80,1024]{1,0:T(8,128)S(1)}, f32[80,1024]{1,0:T(8,128)S(1)}, u32[]{:S(2)}, u32[]{:S(2)}) collective-permute-start(f32[80,1024]{1,0:T(8,128)S(1)} %copy-done.71), channel_id=1, source_target_pairs={{0,12},{1,13},{2,14},{3,15},{4,0},{5,1},{6,2},{7,3},{8,4},{9,5},{1... | collective-permute-start | bytes 983048 | tf_op jit(solution)/shard_map/cond/branch_0_fun/ppermute | solution.py:491
  414.1 33.2 %copy-start.24 = (f32[80,1024]{1,0:T(8,128)S(1)}, f32[80,1024]{1,0:T(8,128)}, u32[]{:S(2)}) copy-start(f32[80,1024]{1,0:T(8,128)} %get-tuple-element.126.refs_4_) | copy-start | bytes 983044
  414.1 24.4 %collective-permute-start.7 = (f32[80,1024]{1,0:T(8,128)}, f32[80,1024]{1,0:T(8,128)S(1)}, u32[]{:S(2)}, u32[]{:S(2)}) collective-permute-start(f32[80,1024]{1,0:T(8,128)} %get-tuple-element.127), channel_id=1, source_target_pairs={{0,4},{1,5},{2,6},{3,7},{4,8},{5,9},{6,10},{7,11},{8,12},{9,13},{1... | collective-permute-start | bytes 983048 | tf_op jit(solution)/shard_map/cond/branch_0_fun/ppermute | solution.py:491
  415.4 29.1 %collective-permute-start.8 = (f32[80,1024]{1,0:T(8,128)}, f32[80,1024]{1,0:T(8,128)S(1)}, u32[]{:S(2)}, u32[]{:S(2)}) collective-permute-start(f32[80,1024]{1,0:T(8,128)} %get-tuple-element.128), channel_id=1, source_target_pairs={{0,8},{1,9},{2,10},{3,11},{4,12},{5,13},{6,14},{7,15},{8,0},{9,1},... | collective-permute-start | bytes 983048 | tf_op jit(solution)/shard_map/cond/branch_0_fun/ppermute | solution.py:491
  417.8 29.5 %collective-permute-start.9 = (f32[80,1024]{1,0:T(8,128)}, f32[80,1024]{1,0:T(8,128)S(1)}, u32[]{:S(2)}, u32[]{:S(2)}) collective-permute-start(f32[80,1024]{1,0:T(8,128)} %get-tuple-element.129), channel_id=1, source_target_pairs={{0,12},{1,13},{2,14},{3,15},{4,0},{5,1},{6,2},{7,3},{8,4},{9,5},{1... | collective-permute-start | bytes 983048 | tf_op jit(solution)/shard_map/cond/branch_0_fun/ppermute | solution.py:491
  421.5 107.0 %collective-permute-start.11 = (f32[384,1024]{1,0:T(8,128)}, f32[384,1024]{1,0:T(8,128)S(1)}, u32[]{:S(2)}, u32[]{:S(2)}) collective-permute-start(f32[384,1024]{1,0:T(8,128)} %slice_add_fusion.1), channel_id=1, source_target_pairs={{0,2},{1,3},{2,0},{3,1},{4,6},{5,7},{6,4},{7,5},{8,10},{9,11},{10,... | collective-permute-start | bytes 4718600 | tf_op jit(solution)/shard_map/cond/branch_0_fun/ppermute | solution.py:488
  433.0 123.0 %collective-permute-start.16 = (f32[384,1024]{1,0:T(8,128)}, f32[384,1024]{1,0:T(8,128)}, u32[]{:S(2)}, u32[]{:S(2)}) collective-permute-start(f32[384,1024]{1,0:T(8,128)} %slice_add_fusion), channel_id=1, source_target_pairs={{0,2},{1,3},{2,0},{3,1},{4,6},{5,7},{6,4},{7,5},{8,10},{9,11},{10,... | collective-permute-start | bytes 4718600 | tf_op jit(solution)/shard_map/cond/branch_0_fun/ppermute | solution.py:488
  526.1 2.3 copy-start.2
  528.4 1.1 copy-start.44
  534.3 30.8 %collective-permute-start.12 = (f32[128,1024]{1,0:T(8,128)}, f32[128,1024]{1,0:T(8,128)S(1)}, u32[]{:S(2)}, u32[]{:S(2)}) collective-permute-start(f32[128,1024]{1,0:T(8,128)} %get-tuple-element.142), channel_id=1, source_target_pairs={{0,4},{1,5},{2,6},{3,7},{4,8},{5,9},{6,10},{7,11},{8,12},{9,13},{1... | collective-permute-start | bytes 1572872 | tf_op jit(solution)/shard_map/cond/branch_0_fun/ppermute | solution.py:491
  553.7 35.9 %collective-permute-start.13 = (f32[128,1024]{1,0:T(8,128)}, f32[128,1024]{1,0:T(8,128)S(1)}, u32[]{:S(2)}, u32[]{:S(2)}) collective-permute-start(f32[128,1024]{1,0:T(8,128)} %get-tuple-element.143), channel_id=1, source_target_pairs={{0,8},{1,9},{2,10},{3,11},{4,12},{5,13},{6,14},{7,15},{8,0},{9,1},... | collective-permute-start | bytes 1572872 | tf_op jit(solution)/shard_map/cond/branch_0_fun/ppermute | solution.py:491
  556.0 57.8 %collective-permute-start.14 = (f32[128,1024]{1,0:T(8,128)}, f32[128,1024]{1,0:T(8,128)S(1)}, u32[]{:S(2)}, u32[]{:S(2)}) collective-permute-start(f32[128,1024]{1,0:T(8,128)} %get-tuple-element.144), channel_id=1, source_target_pairs={{0,12},{1,13},{2,14},{3,15},{4,0},{5,1},{6,2},{7,3},{8,4},{9,5},{1... | collective-permute-start | bytes 1572872 | tf_op jit(solution)/shard_map/cond/branch_0_fun/ppermute | solution.py:491
  560.7 62.2 %collective-permute-start.17 = (f32[128,1024]{1,0:T(8,128)}, f32[128,1024]{1,0:T(8,128)S(1)}, u32[]{:S(2)}, u32[]{:S(2)}) collective-permute-start(f32[128,1024]{1,0:T(8,128)} %get-tuple-element.149), channel_id=1, source_target_pairs={{0,4},{1,5},{2,6},{3,7},{4,8},{5,9},{6,10},{7,11},{8,12},{9,13},{1... | collective-permute-start | bytes 1572872 | tf_op jit(solution)/shard_map/cond/branch_0_fun/ppermute | solution.py:491
  562.7 71.4 %collective-permute-start.18 = (f32[128,1024]{1,0:T(8,128)}, f32[128,1024]{1,0:T(8,128)}, u32[]{:S(2)}, u32[]{:S(2)}) collective-permute-start(f32[128,1024]{1,0:T(8,128)} %get-tuple-element.150), channel_id=1, source_target_pairs={{0,8},{1,9},{2,10},{3,11},{4,12},{5,13},{6,14},{7,15},{8,0},{9,1},... | collective-permute-start | bytes 1572872 | tf_op jit(solution)/shard_map/cond/branch_0_fun/ppermute | solution.py:491
  565.1 70.4 %copy-start.7 = (f32[128,1024]{1,0:T(8,128)S(1)}, f32[128,1024]{1,0:T(8,128)}, u32[]{:S(2)}) copy-start(f32[128,1024]{1,0:T(8,128)} %get-tuple-element.141.refs_0_) | copy-start | bytes 1572868
  565.1 70.4 %copy-start.9 = (f32[128,1024]{1,0:T(8,128)S(1)}, f32[128,1024]{1,0:T(8,128)}, u32[]{:S(2)}) copy-start(f32[128,1024]{1,0:T(8,128)} %get-tuple-element.148.refs_4_) | copy-start | bytes 1572868
  565.1 70.4 %collective-permute-start.19 = (f32[128,1024]{1,0:T(8,128)}, f32[128,1024]{1,0:T(8,128)}, u32[]{:S(2)}, u32[]{:S(2)}) collective-permute-start(f32[128,1024]{1,0:T(8,128)} %get-tuple-element.151), channel_id=1, source_target_pairs={{0,12},{1,13},{2,14},{3,15},{4,0},{5,1},{6,2},{7,3},{8,4},{9,5},{1... | collective-permute-start | bytes 1572872 | tf_op jit(solution)/shard_map/cond/branch_0_fun/ppermute | solution.py:491
  574.8 64.4 %copy-start.30 = (f32[128,2048]{1,0:T(8,128)S(1)}, f32[128,2048]{1,0:T(8,128)}, u32[]{:S(2)}) copy-start(f32[128,2048]{1,0:T(8,128)} %fusion.19) | copy-start | bytes 3145732
  647.9 0.8 copy-start.49
